TPU v7x, 32 devices: a whole 2x2x4 slice. The times are simulated.
32 devices in a mesh: ctx: 16 (over z, y, core), head: 2 (over x).
Axes of the slice: x: 2, y: 2, z: 4, core: 2. Of those that a mesh axis runs over, the one named last changes fastest.
Arguments:
- queries: bfloat16 [16, 1024, 2048], P('ctx', None, 'head'), may hold values from -8 to 8
- keys: bfloat16 [16, 1024, 2048], P('ctx', None, 'head'), may hold values from -8 to 8
- values: bfloat16 [16, 1024, 2048], P('ctx', None, 'head'), may hold values from -24 to 24
- w_out: bfloat16 [2048, 4096], P('head'), may hold values from -0.125 to 0.125
Outputs:
- mixed: bfloat16 [16, 1024, 4096], P('ctx', 'head')
All inputs are finite; a program needn't handle non-finite values.
Results may differ from a plain program's by a relative error of at most 0.013.
Values may be sent and summed in bfloat16 or wider, within the bound.
A program may use at most 128 MiB of HBM per device.

v0:
```python
import functools

import jax
import jax.numpy as jnp
from jax import lax
from jax.experimental import pallas as pl
from jax.experimental.pallas import tpu as pltpu
from jax.sharding import PartitionSpec as P

HD = 128
GROUP = 4
MESH = pl.DeviceIdType.MESH
PIECES = 8
STRAIGHT = 2
PARTS = 2

masked_score = -1e30


def attend(query, key, value, allowed):
    scores = lax.dot_general(
        query, key, (((1,), (1,)), ((), ())), preferred_element_type=jnp.float32
    ) * jnp.float32(1.0 / HD**0.5)
    scores = jnp.where(allowed, scores, masked_score)
    top = jnp.max(scores, axis=-1, keepdims=True)
    expo = jnp.exp(scores - top)
    total = jnp.sum(expo, axis=-1, keepdims=True)
    mixed = jnp.dot(expo.astype(jnp.bfloat16), value, preferred_element_type=jnp.float32)
    return (mixed / total).astype(jnp.bfloat16)


def body(
    n, q_hbm, k_hbm, v_hbm, w_hbm, out_ref, q_row, k_row, v_row, q_col, k_col, v_col,
    col_out, row_out, joined, summed, w_own, w_other, local_sem, in_send, in_recv, back_send, back_recv,
    w_send, w_recv, row_send, row_recv,
):
    me, head = lax.axis_index("ctx"), lax.axis_index("head")
    other = 1 - head
    stride = q_hbm.shape[1]
    block = q_row.shape[1]
    depth = w_own.shape[0]
    half = joined.shape[1]
    cols = stride // n
    share = block // PARTS
    hbm = (q_hbm, k_hbm, v_hbm)
    rows_in = (q_row, k_row, v_row)
    cols_in = (q_col, k_col, v_col)
    back_head = lax.div(me * cols, half)
    member = lax.rem(me, 4)
    sibling = me + 1 - 2 * lax.rem(me, 2)
    beside = me + 2 - 4 * lax.div(member, 2)
    piece = depth // (4 * PIECES)

    def col_copy(t, part, d):
        peer = lax.rem(me + d, n)
        lanes = pl.ds(part * share, share)
        return pltpu.make_async_remote_copy(
            src_ref=hbm[t].at[0, pl.ds(peer * cols, cols), pl.ds(block + part * share, share)],
            dst_ref=cols_in[t].at[me, :, lanes],
            send_sem=in_send.at[t * PARTS + part, d],
            recv_sem=in_recv.at[t * PARTS + part, d],
            device_id=(peer, head),
            device_id_type=MESH,
        )

    def col_arrival(t, part, d):
        source = lax.rem(me + n - d, n)
        lanes = pl.ds(part * share, share)
        return pltpu.make_async_remote_copy(
            src_ref=hbm[t].at[0, pl.ds(0, cols), pl.ds(block + part * share, share)],
            dst_ref=cols_in[t].at[source, :, lanes],
            send_sem=in_send.at[t * PARTS + part, d],
            recv_sem=in_recv.at[t * PARTS + part, d],
            device_id=(source, head),
            device_id_type=MESH,
        )

    def w_copy(source, index, way, to_ctx, to_head):
        rows = pl.ds(index * piece, piece)
        return pltpu.make_async_remote_copy(
            src_ref=source.at[rows],
            dst_ref=w_other.at[rows],
            send_sem=w_send.at[way, index],
            recv_sem=w_recv.at[index],
            device_id=(to_ctx, to_head),
            device_id_type=MESH,
        )

    def index_of(who, s):
        return who * PIECES + s

    member_sibling = lax.rem(sibling, 4)
    member_beside = lax.rem(beside, 4)
    member_far = lax.rem(member + 2, 4) + 1 - 2 * lax.rem(member, 2)

    for part in range(PARTS):

        @pl.loop(1, n)
        def _(d):
            for t in range(3):
                col_copy(t, part, d).start()

    @pl.loop(0, PIECES)
    def _(s):
        w_copy(w_hbm, index_of(member, s), 0, me, other).start()

    @pl.loop(PIECES - STRAIGHT, PIECES)
    def _(s):
        w_copy(w_hbm, index_of(member_beside, s), 0, me, other).start()

    local = [
        pltpu.make_async_copy(hbm[t].at[0, :, pl.ds(0, block)], rows_in[t], local_sem.at[t])
        for t in range(3)
    ]
    local += [
        pltpu.make_async_copy(
            hbm[t].at[0, pl.ds(me * cols, cols), pl.ds(block, block)],
            cols_in[t].at[me],
            local_sem.at[3 + t],
        )
        for t in range(3)
    ]
    local.append(pltpu.make_async_copy(w_hbm, w_own, local_sem.at[6]))
    for copy in local:
        copy.start()
    for copy in local[:3]:
        copy.wait()

    tile = min(256, half)
    row_index = lax.broadcasted_iota(jnp.int32, (tile, stride), 0)
    key_index = lax.broadcasted_iota(jnp.int32, (tile, stride), 1)

    @pl.loop(0, block // HD)
    def _(h):
        lanes = pl.ds(pl.multiple_of(h * HD, HD), HD)
        for start in range(0, stride, tile):
            end = start + tile
            row_out[pl.ds(start, tile), lanes] = attend(
                q_row[pl.ds(start, tile), lanes],
                k_row[pl.ds(0, end), lanes],
                v_row[pl.ds(0, end), lanes],
                key_index[:, :end] <= row_index[:, :end] + start,
            )

    row_copy = pltpu.make_async_remote_copy(
        src_ref=row_out.at[pl.ds(pl.multiple_of(other * half, half), half)],
        dst_ref=joined.at[head, :, pl.ds(0, block)],
        send_sem=row_send,
        recv_sem=row_recv,
        device_id=(me, other),
        device_id_type=MESH,
    )
    row_copy.start()
    joined[head, :, pl.ds(0, block)] = row_out[pl.ds(pl.multiple_of(head * half, half), half)]

    def onward(first, last):
        @pl.loop(first, last)
        def _(s):
            index = index_of(member, s)
            w_copy(w_hbm, index, 0, me, other).wait_recv()

            @pl.when(s < PIECES - STRAIGHT)
            def _():
                w_copy(w_other, index, 1, beside, head).start()

            w_copy(w_other, index, 2, sibling, head).start()

    onward(0, PIECES // 2)

    for copy in local[3:]:
        copy.wait()

    step = 512

    def tiles(add):
        @pl.loop(0, out_ref.shape[1] // step)
        def _(c):
            add(pl.ds(pl.multiple_of(c * step, step), step))

    def own_row_part(lanes):
        summed[:, lanes] = jnp.dot(
            joined[head, :, pl.ds(0, block)],
            w_own[pl.ds(0, block), lanes],
            preferred_element_type=jnp.float32,
        )

    tiles(own_row_part)
    width = min(cols, max(16, 256 // n))
    size = n * width
    r_index = lax.broadcasted_iota(jnp.int32, (size, size), 0)
    s_index = lax.broadcasted_iota(jnp.int32, (size, size), 1)
    allowed = (s_index <= r_index) & (((r_index - s_index) & (width - 1)) == 0)

    slot_here = lax.rem(me, n // 2)
    stays = back_head == head

    def landing(source_head, part, slot):
        return joined.at[
            source_head,
            pl.ds(pl.multiple_of(slot * cols, cols), cols),
            pl.ds(block + part * share, share),
        ]

    def back_copy(part, r):
        return pltpu.make_async_remote_copy(
            src_ref=col_out.at[r, :, pl.ds(part * share, share)],
            dst_ref=landing(head, part, slot_here),
            send_sem=back_send.at[part, r],
            recv_sem=back_recv.at[head * PARTS + part, slot_here],
            device_id=(r, back_head),
            device_id_type=MESH,
        )

    def back_arrival(source_head, part, slot):
        return pltpu.make_async_remote_copy(
            src_ref=col_out.at[0, :, pl.ds(part * share, share)],
            dst_ref=landing(source_head, part, slot),
            send_sem=back_send.at[part, 0],
            recv_sem=back_recv.at[source_head * PARTS + part, slot],
            device_id=(me, other),
            device_id_type=MESH,
        )

    for part in range(PARTS):

        @pl.loop(1, n)
        def _(d):
            for t in range(3):
                col_arrival(t, part, d).wait_recv()

        @pl.loop(part * (share // HD), (part + 1) * (share // HD))
        def _(h):
            lanes = pl.ds(pl.multiple_of(h * HD, HD), HD)
            for start in range(0, cols, width):
                at = (slice(None), pl.ds(start, width), lanes)
                got = attend(*(ref[at].reshape(size, HD) for ref in cols_in), allowed)
                col_out[at] = got.reshape(n, width, HD)

        @pl.loop(1, n)
        def _(d):
            back_copy(part, lax.rem(me + d, n)).start()

        @pl.when(stays)
        def _():
            rows = pl.ds(pl.multiple_of(slot_here * cols, cols), cols)
            joined[head, rows, pl.ds(block + part * share, share)] = col_out[
                me, :, pl.ds(part * share, share)
            ]

        @pl.when(jnp.logical_not(stays))
        def _():
            back_copy(part, me).start()

        if part == 0:
            onward(PIECES // 2, PIECES)

    @pl.loop(0, PIECES)
    def _(s):
        index = index_of(member_beside, s)
        w_copy(w_other, index, 1, beside, head).wait_recv()
        w_copy(w_other, index, 3, sibling, head).start()

    row_copy.wait_recv()

    def back_wait(source_head):
        @pl.loop(0, n // 2)
        def _(slot):
            mine = (head * (n // 2) + slot == me) & (head == source_head)

            @pl.when(jnp.logical_not(mine))
            def _():
                for part in range(PARTS):
                    back_arrival(source_head, part, slot).wait_recv()

    back_wait(head)

    def own_col_part(lanes):
        summed[:, lanes] += jnp.dot(
            joined[head, :, pl.ds(block, block)],
            w_own[pl.ds(block, block), lanes],
            preferred_element_type=jnp.float32,
        )

    tiles(own_col_part)

    @pl.loop(0, PIECES)
    def _(s):
        w_copy(w_other, index_of(member_sibling, s), 2, sibling, head).wait_recv()
        w_copy(w_other, index_of(member_far, s), 3, sibling, head).wait_recv()

    back_wait(other)

    def other_part(lanes):
        total = summed[:, lanes] + jnp.dot(
            joined[other], w_other[:, lanes], preferred_element_type=jnp.float32
        )
        out_ref[:, lanes] = total.astype(jnp.bfloat16)

    tiles(other_part)

    for part in range(PARTS):

        @pl.loop(1, n)
        def _(d):
            for t in range(3):
                col_copy(t, part, d).wait_send()

    @pl.loop(0, PIECES)
    def _(s):
        w_copy(w_hbm, index_of(member, s), 0, me, other).wait_send()
        w_copy(w_other, index_of(member, s), 2, sibling, head).wait_send()
        w_copy(w_other, index_of(member_beside, s), 3, sibling, head).wait_send()

    @pl.loop(0, PIECES - STRAIGHT)
    def _(s):
        w_copy(w_other, index_of(member, s), 1, beside, head).wait_send()

    @pl.loop(PIECES - STRAIGHT, PIECES)
    def _(s):
        w_copy(w_hbm, index_of(member_beside, s), 0, me, other).wait_send()

    row_copy.wait_send()

    for part in range(PARTS):

        @pl.loop(1, n)
        def _(d):
            back_copy(part, lax.rem(me + d, n)).wait_send()

        @pl.when(jnp.logical_not(stays))
        def _():
            back_copy(part, me).wait_send()


def on_device(n, queries, keys, values, w_out):
    _, stride, local_feat = queries.shape
    depth, model_width = w_out.shape
    block = GROUP * HD
    assert queries.shape[0] == 1 and local_feat == 2 * block
    half = stride // lax.axis_size("head")
    cols = stride // n
    bf16 = jnp.bfloat16
    dma = pltpu.SemaphoreType.DMA
    out = pl.pallas_call(
        functools.partial(body, n),
        out_shape=jax.ShapeDtypeStruct((half, model_width), bf16),
        in_specs=[pl.BlockSpec(memory_space=pltpu.HBM)] * 4,
        out_specs=pl.BlockSpec(memory_space=pltpu.VMEM),
        scratch_shapes=[pltpu.VMEM((stride, block), bf16)] * 3
        + [pltpu.VMEM((n, cols, block), bf16)] * 4
        + [
            pltpu.VMEM((stride, block), bf16),
            pltpu.VMEM((2, half, local_feat), bf16),
            pltpu.VMEM((half, model_width), jnp.float32),
            pltpu.VMEM((depth, model_width), bf16),
            pltpu.VMEM((depth, model_width), bf16),
            dma((7,)),
            dma((3 * PARTS, n)),
            dma((3 * PARTS, n)),
            dma((PARTS, n)),
            dma((2 * PARTS, n // 2)),
            dma((4, 4 * PIECES)),
            dma((4 * PIECES,)),
            dma,
            dma,
        ],
        compiler_params=pltpu.CompilerParams(has_side_effects=True, vmem_limit_bytes=60 * 2**20),
    )(queries, keys, values, w_out)
    return out.reshape((1, half, model_width))


def solution(mesh):
    return jax.shard_map(
        functools.partial(on_device, mesh.shape["ctx"]),
        mesh=mesh,
        in_specs=(
            P("ctx", None, "head"),
            P("ctx", None, "head"),
            P("ctx", None, "head"),
            P("head", None),
        ),
        out_specs=P("ctx", "head", None),
        check_vma=False,
    )
```

profile of v0, /device:TPU:25, one launch (start us, length us, event | category | flops | bytes accessed | tf_op | source)
XLA Modules:
  0.0 118.7 jit_solution(2681369314071166058)
XLA Ops:
  0.0 114.0 %shard_map.46 = bf16[512,4096]{1,0:T(8,128)(2,1)} custom-call(bf16[1,1024,1024]{2,1,0:T(8,128)(2,1)} %q_hbm.1, bf16[1,1024,1024]{2,1,0:T(8,128)(2,1)} %k_hbm.1, bf16[1,1024,1024]{2,1,0:T(8,128)(2,1)} %v_hbm.1, bf16[1024,4096]{1,0:T(8,128)(2,1)} %w_hbm.1), custom_call_target="tpu_custom_call" | custom-call | tf_op jit(solution)/shard_map/pallas_call | solution.py:344
  114.0 4.7 %copy.6 = bf16[1,512,4096]{2,1,0:T(8,128)(2,1)} copy(bf16[1,512,4096]{2,1,0:T(8,128)(2,1)} %bitcast.1) | data formatting | bytes 8388608
where the time goes:
time: 121 us; the launch traced here: 119 us
  Pallas kernels  114 us (94%)
  local copies, waits for them, and re-layouts  4.7 us (4%)
    pallas_call x1, Pallas kernels, on_device(): pl.pallas_call(functools.partial(body, n), out_shape=jax.ShapeDtypeStruct...  114 us
    unnamed x1, local copies, waits for them, and re-layouts  4.7 us

commit v1 on v0

--- a/solution.py
+++ b/solution.py
@@ -10,9 +10,14 @@
 HD = 128
 GROUP = 4
 MESH = pl.DeviceIdType.MESH
-PIECES = 8
+SHARES = 8
 STRAIGHT = 2
 PARTS = 2
+LAYER = 4
+CHUNKS = 8
+WIDTH = 16
+PIECES = 4
+AHEAD = 2
 
 masked_score = -1e30
 
@@ -27,6 +32,621 @@
     total = jnp.sum(expo, axis=-1, keepdims=True)
     mixed = jnp.dot(expo.astype(jnp.bfloat16), value, preferred_element_type=jnp.float32)
     return (mixed / total).astype(jnp.bfloat16)
+
+
+def weigh(query, key, value, allowed):
+    scores = lax.dot_general(
+        query, key, (((1,), (1,)), ((), ())), preferred_element_type=jnp.float32
+    ) * jnp.float32(1.0 / HD**0.5)
+    if allowed is not None:
+        scores = jnp.where(allowed, scores, masked_score)
+    top = jnp.max(scores, axis=-1, keepdims=True)
+    expo = jnp.exp(scores - top)
+    total = jnp.sum(expo, axis=-1, keepdims=True)
+    mixed = jnp.dot(expo.astype(jnp.bfloat16), value, preferred_element_type=jnp.float32)
+    return (mixed / total).astype(jnp.bfloat16), top + jnp.log(total)
+
+
+def layered(
+    n, q_hbm, k_hbm, v_hbm, w_hbm, out_hbm, q_row, k_row, v_row, q_in, k_in, v_in, o_out, p_in,
+    stats, stats_in, row_out, joined, summed, w_own, w_other, staged,
+    local_sem, lay_send, lay_recv, up_send, up_recv, part_send, part_recv, stat_send, stat_recv,
+    back_send, back_recv, w_send, w_recv, row_send, row_recv, out_sem,
+):
+    me, head = lax.axis_index("ctx"), lax.axis_index("head")
+    other = 1 - head
+    z, s = lax.div(me, LAYER), lax.rem(me, LAYER)
+    core = lax.rem(s, 2)
+    sib = s + 1 - 2 * core
+    opp = s + 2 - 4 * lax.div(s, 2)
+    far = sib + 2 - 4 * lax.div(sib, 2)
+    peers = (s, sib, opp, far)
+    stride = q_hbm.shape[1]
+    block = q_row.shape[1]
+    depth = w_own.shape[0]
+    half = joined.shape[1]
+    cols = stride // LAYER
+    cw = cols // CHUNKS
+    per = half // cols
+    hbm = (q_hbm, k_hbm, v_hbm)
+    ins = (q_in, k_in, v_in)
+    own_at = (0, LAYER, LAYER)
+    back_head = lax.div(s * cols, half)
+    back_start = lax.rem(s * cols, half)
+    stays = back_head == head
+    feats = pl.ds(block, block)
+
+    def remote(src, dst, send, recv, ctx, at):
+        return pltpu.make_async_remote_copy(
+            src_ref=src, dst_ref=dst, send_sem=send, recv_sem=recv,
+            device_id=(ctx, at), device_id_type=MESH,
+        )
+
+    def here(slot):
+        return z * LAYER + slot
+
+    def lay(t, j, d, source):
+        row = peers[d] if source else s
+        return remote(
+            hbm[t].at[0, pl.ds(peers[d] * cols + j * cw, cw), feats],
+            ins[t].at[own_at[t] + row, pl.ds(j * cw, cw)],
+            lay_send.at[t * CHUNKS + j, d], lay_recv.at[t * CHUNKS + j, d],
+            here(peers[d]), head,
+        )
+
+    def up(kind, t, j, d, layer, base):
+        if d < 2:
+            src, slot, row = hbm[t].at[0, pl.ds(peers[d] * cols + j * cw, cw), feats], peers[d], s
+        else:
+            src, slot, row = ins[t].at[own_at[t] + peers[d], pl.ds(j * cw, cw)], s, peers[d]
+        return remote(
+            src, ins[t].at[base + row, pl.ds(j * cw, cw)],
+            up_send.at[kind * CHUNKS + j, d], up_recv.at[kind * CHUNKS + j, d],
+            layer * LAYER + slot, head,
+        )
+
+    def up_arrival(kind, t, j, d, base):
+        return remote(
+            hbm[t].at[0, pl.ds(0, cw), feats], ins[t].at[base + peers[d], pl.ds(j * cw, cw)],
+            up_send.at[kind * CHUNKS + j, d], up_recv.at[kind * CHUNKS + j, d],
+            here(sib), head,
+        )
+
+    routes = {
+        0: ((0, 1, 1, 0), (1, 2, 1, 0)),
+        2: ((2, 0, 1, LAYER),),
+        3: ((3, 0, 1, 2 * LAYER), (2, 0, 2, LAYER)),
+    }
+
+    def direct(layer, j):
+        for kind, t, to, base in routes[layer]:
+            for d in (0, 1):
+                up(kind, t, j, d, to, base).start()
+
+    def relay(layer, j):
+        for t in sorted({t for _, t, _, _ in routes[layer]}):
+            for d in (2, 3):
+                lay(t, j, d, True).wait_recv()
+                for kind, t2, to, base in routes[layer]:
+                    if t2 == t:
+                        up(kind, t, j, d, to, base).start()
+
+    def piece_rows(q, c, k):
+        eighth = depth // 16
+        rows = eighth // (PIECES // 2)
+        start = lax.div(k, PIECES // 2) * (depth // 2)
+        start += (q * 2 + c) * eighth + lax.rem(k, PIECES // 2) * rows
+        return pl.ds(start, rows)
+
+    def w_copy(source, q, c, k, way, to_ctx, to_head):
+        rows = piece_rows(q, c, k)
+        index = (q * 2 + c) * PIECES + k
+        return remote(
+            source.at[rows], w_other.at[rows], w_send.at[way, index], w_recv.at[index], to_ctx, to_head
+        )
+
+    even = lax.rem(z + lax.div(s, 2), 2)
+    y_next = here(opp)
+    z_next = me + LAYER - 2 * LAYER * lax.rem(z, 2)
+    z_early = (z == 1) | (z == 2)
+
+    def w_first(q, k):
+        return w_copy(w_hbm, 2 * even + q, core, k, 0, me, other)
+
+    def w_side(q, k):
+        return w_copy(w_other, 2 * even + q, core, k, 2, y_next if q == 0 else z_next, head)
+
+    def w_beside(q, k):
+        return w_copy(w_other, 2 * (1 - even) + q, core, k, 1, here(sib), head)
+
+    def w_here(q, k):
+        return w_copy(w_other, 2 * even + q, core, k, 1, here(sib), head)
+
+    def w_in(q, k):
+        w_first(q, k).wait_recv()
+        w_here(q, k).start()
+        if q == 0:
+            w_side(q, k).start()
+        else:
+
+            @pl.when(z_early)
+            def _():
+                w_side(q, k).start()
+
+    def w_on(q, k):
+        w_copy(w_other, 2 * (1 - even) + q, core, k, 2, me, other).wait_recv()
+        w_beside(q, k).start()
+
+    def exchange(ts):
+        @pl.loop(0, CHUNKS)
+        def _(j):
+            for t in ts:
+                for d in (2, 3, 1):
+                    lay(t, j, d, False).start()
+
+    for layer in routes:
+
+        @pl.when(z == layer)
+        def _():
+            for j in range(AHEAD):
+                direct(layer, j)
+
+    @pl.when(z < 2)
+    def _():
+        exchange((1, 2))
+        exchange((0,))
+
+    @pl.when(z >= 2)
+    def _():
+        exchange((0,))
+        exchange((1, 2))
+
+    @pl.loop(0, PIECES)
+    def _(k):
+        w_first(0, k).start()
+        w_first(1, k).start()
+
+    local = [
+        pltpu.make_async_copy(hbm[t].at[0, :, pl.ds(0, block)], (q_row, k_row, v_row)[t], local_sem.at[t])
+        for t in range(3)
+    ]
+    local += [
+        pltpu.make_async_copy(
+            hbm[t].at[0, pl.ds(s * cols, cols), feats], ins[t].at[own_at[t] + s], local_sem.at[3 + t]
+        )
+        for t in range(3)
+    ]
+    local.append(pltpu.make_async_copy(w_hbm, w_own, local_sem.at[6]))
+    for copy in local:
+        copy.start()
+    for copy in local[:6]:
+        copy.wait()
+
+    tile = min(256, half)
+    row_index = lax.broadcasted_iota(jnp.int32, (tile, stride), 0)
+    key_index = lax.broadcasted_iota(jnp.int32, (tile, stride), 1)
+
+    def row_tile(h, start):
+        lanes = pl.ds(pl.multiple_of(h * HD, HD), HD)
+        end = start + tile
+        row_out[pl.ds(start, tile), lanes] = attend(
+            q_row[pl.ds(start, tile), lanes],
+            k_row[pl.ds(0, end), lanes],
+            v_row[pl.ds(0, end), lanes],
+            key_index[:, :end] <= row_index[:, :end] + start,
+        )
+
+    def spread(sums, size, off):
+        lane = lax.broadcasted_iota(jnp.int32, (size, HD), 1)
+        row = lax.broadcasted_iota(jnp.int32, (size, HD), 0)
+        return jnp.sum(jnp.where(lane == row + off, sums, 0.0), axis=0, keepdims=True)
+
+    def column(line, size, off):
+        lane = lax.broadcasted_iota(jnp.int32, (size, HD), 1)
+        row = lax.broadcasted_iota(jnp.int32, (size, HD), 0)
+        return jnp.sum(jnp.where(lane == row + off, line, 0.0), axis=1, keepdims=True)
+
+    heads = block // HD
+    size = LAYER * WIDTH
+
+    def small(q_at, q_rows, k_at, k_rows, c, b, causal, keep):
+        start = pl.multiple_of(c * cw + b * WIDTH, WIDTH)
+        shape = (q_rows * WIDTH, k_rows * WIDTH)
+        r = lax.broadcasted_iota(jnp.int32, shape, 0)
+        m = lax.broadcasted_iota(jnp.int32, shape, 1)
+        allowed = ((r - m) & (WIDTH - 1)) == 0
+        if causal is not None:
+            allowed &= m <= r + causal * WIDTH
+        for h in range(heads):
+            lanes = pl.ds(h * HD, HD)
+            q_slice = (pl.ds(q_at, q_rows), pl.ds(start, WIDTH), lanes)
+            k_slice = (pl.ds(k_at, k_rows), pl.ds(start, WIDTH), lanes)
+            got, sums = weigh(
+                q_in[q_slice].reshape(shape[0], HD),
+                k_in[k_slice].reshape(shape[1], HD),
+                v_in[k_slice].reshape(shape[1], HD),
+                allowed,
+            )
+            o_out[q_slice] = got.reshape(q_rows, WIDTH, HD)
+            if keep is not None:
+                stats[c * (cw // WIDTH) + b, pl.ds(h, 1)] = spread(sums, shape[0], keep)
+
+    strips = cw // WIDTH
+
+    def partial(kind, slot, j, rows, layer, base):
+        return remote(
+            o_out.at[pl.ds(rows, LAYER), pl.ds(j * cw, cw)],
+            p_in.at[pl.ds(base, LAYER), pl.ds(j * cw, cw)],
+            part_send.at[kind, j], part_recv.at[slot, j], layer * LAYER + s, head,
+        )
+
+    def partial_stats(kind, slot, j, layer):
+        at = pl.ds(j * strips, strips)
+        return remote(
+            stats.at[at], stats_in.at[slot, at],
+            stat_send.at[kind, j], stat_recv.at[slot, j], layer * LAYER + s, head,
+        )
+
+    def back(j, d):
+        row = peers[d]
+        return remote(
+            o_out.at[row, pl.ds(j * cw, cw)],
+            joined.at[head, pl.ds(back_start + j * cw, cw), feats],
+            back_send.at[j, d], back_recv.at[head * per + lax.rem(s, per), j],
+            here(row), back_head,
+        )
+
+    def back_all(j):
+        for d in (2, 3, 1):
+            back(j, d).start()
+
+        @pl.when(jnp.logical_not(stays))
+        def _():
+            back(j, 0).start()
+
+        @pl.when(stays)
+        def _():
+            joined[head, pl.ds(pl.multiple_of(back_start + j * cw, WIDTH), cw), feats] = o_out[
+                s, pl.ds(pl.multiple_of(j * cw, WIDTH), cw)
+            ]
+
+    def ext(j):
+        for t in (1, 2):
+            for d in (1, 2, 3):
+                lay(t, j, d, True).wait_recv()
+        for kind, t, base in ((0, 1, 0), (1, 2, 0), (2, 0, LAYER), (3, 0, 2 * LAYER)):
+            for d in range(4):
+                up_arrival(kind, t, j, d, base).wait_recv()
+        for b in range(strips):
+            small(LAYER, 2 * LAYER, 0, 2 * LAYER, j, b, None, 0)
+        for kind, rows, layer in ((0, LAYER, 2), (1, 2 * LAYER, 3)):
+            partial(kind, 0, j, rows, layer, 0).start()
+            partial_stats(kind, 0, j, layer).start()
+
+    def own(c):
+        @pl.when(z == 0)
+        def _():
+            for t, ds in ((0, (1, 2, 3)), (1, (1,)), (2, (1,))):
+                for d in ds:
+                    lay(t, c, d, True).wait_recv()
+            for b in range(strips):
+                small(0, LAYER, LAYER, LAYER, c, b, 0, None)
+            back_all(c)
+
+        @pl.when(z == 1)
+        def _():
+            for d in (1, 2, 3):
+                lay(0, c, d, True).wait_recv()
+            for b in range(strips):
+                small(0, LAYER, 0, 2 * LAYER, c, b, LAYER, None)
+            back_all(c)
+
+        @pl.when(z >= 2)
+        def _():
+            lay(0, c, 1, True).wait_recv()
+            for t in (1, 2):
+                for d in (1, 2, 3):
+                    lay(t, c, d, True).wait_recv()
+
+        @pl.when(z == 2)
+        def _():
+            for d in range(4):
+                up_arrival(2, 0, c, d, LAYER).wait_recv()
+            for b in range(strips):
+                small(0, 2 * LAYER, LAYER, LAYER, c, b, 0, 0)
+            partial(0, 1, c, LAYER, 3, LAYER).start()
+            partial_stats(0, 1, c, 3).start()
+
+        @pl.when(z == 3)
+        def _():
+            for b in range(strips):
+                small(0, LAYER, LAYER, LAYER, c, b, 0, size)
+
+    def combine(c):
+        def weights(lines):
+            top = functools.reduce(jnp.maximum, lines)
+            terms = [jnp.exp(line - top) for line in lines]
+            total = functools.reduce(jnp.add, terms)
+            return [term / total for term in terms]
+
+        def mix(b, lines, off):
+            start = pl.multiple_of(c * cw + b * WIDTH, WIDTH)
+            shares = weights(lines)
+            for h in range(heads):
+                lanes = pl.ds(h * HD, HD)
+                at = (pl.ds(0, LAYER), pl.ds(start, WIDTH), lanes)
+                parts = [o_out[at], p_in[at]]
+                if len(lines) == 3:
+                    parts.append(p_in[pl.ds(LAYER, LAYER), pl.ds(start, WIDTH), lanes])
+                total = 0.0
+                for part, share in zip(parts, shares):
+                    weight = column(share[h : h + 1], size, off)
+                    total += part.reshape(size, HD).astype(jnp.float32) * weight
+                o_out[at] = total.astype(jnp.bfloat16).reshape(LAYER, WIDTH, HD)
+
+        def wait(slot):
+            partial(0, slot, c, 0, 0, slot * LAYER).wait_recv()
+            partial_stats(0, slot, c, 0).wait_recv()
+
+        @pl.when(z == 2)
+        def _():
+            wait(0)
+            for b in range(strips):
+                strip = c * strips + b
+                mix(b, [stats[strip, :heads], stats_in[0, strip, :heads]], 0)
+            back_all(c)
+
+        @pl.when(z == 3)
+        def _():
+            wait(0)
+            wait(1)
+            for b in range(strips):
+                strip = c * strips + b
+                mix(
+                    b,
+                    [stats[strip, :heads], stats_in[0, strip, :heads], stats_in[1, strip, :heads]],
+                    size,
+                )
+            back_all(c)
+
+    def step_of(h, u):
+        j = 2 * h + u
+        tiles_of = [start for i, start in enumerate(range(0, stride, tile)) if (i % 4 in (0, 3)) == (u == 0)]
+        for start in tiles_of:
+            row_tile(h, start)
+        for layer in routes:
+
+            @pl.when(z == layer)
+            def _():
+                relay(layer, j)
+
+                @pl.when(j + AHEAD < CHUNKS)
+                def _():
+                    direct(layer, j + AHEAD)
+
+        @pl.when(z == 1)
+        def _():
+            ext(j)
+
+        if u == 0:
+
+            @pl.when(h > 0)
+            def _():
+                w_in(1, h - 1)
+
+        else:
+            w_in(0, h)
+
+        @pl.when(h >= heads // 2)
+        def _():
+            c = 4 * (h - heads // 2) + 2 * u
+            own(c)
+            own(c + 1)
+
+    @pl.loop(0, heads)
+    def _(h):
+        step_of(h, 0)
+        step_of(h, 1)
+
+    row_copy = remote(
+        row_out.at[pl.ds(pl.multiple_of(other * half, half), half)],
+        joined.at[head, :, pl.ds(0, block)], row_send, row_recv, me, other,
+    )
+    row_copy.start()
+    joined[head, :, pl.ds(0, block)] = row_out[pl.ds(pl.multiple_of(head * half, half), half)]
+
+    w_in(1, PIECES - 1)
+
+    @pl.when(jnp.logical_not(z_early))
+    def _():
+        @pl.loop(0, PIECES)
+        def _(k):
+            w_side(1, k).start()
+
+    local[6].wait()
+    step = 512
+    count = staged.shape[1] // step
+
+    def tiles(add):
+        @pl.loop(0, count)
+        def _(c):
+            add(pl.ds(pl.multiple_of(c * step, step), step))
+
+    def own_row_part(lanes):
+        summed[:, lanes] = jnp.dot(
+            joined[head, :, pl.ds(0, block)],
+            w_own[pl.ds(0, block), lanes],
+            preferred_element_type=jnp.float32,
+        )
+
+    tiles(own_row_part)
+
+    @pl.when(z >= 2)
+    def _():
+        @pl.loop(0, CHUNKS - 2)
+        def _(c):
+            combine(c)
+
+    @pl.loop(0, PIECES)
+    def _(k):
+        w_on(0, k)
+
+    @pl.when(z >= 2)
+    def _():
+        @pl.loop(CHUNKS - 2, CHUNKS)
+        def _(c):
+            combine(c)
+
+    @pl.loop(0, PIECES)
+    def _(k):
+        w_on(1, k)
+
+    def w_from_sibling(first, last):
+        @pl.loop(first, last)
+        def _(k):
+            for q in range(4):
+                w_copy(w_other, q, 1 - core, k, 1, here(sib), head).wait_recv()
+
+    w_from_sibling(0, PIECES // 2)
+    row_copy.wait_recv()
+
+    def other_row_part(lanes):
+        summed[:, lanes] += jnp.dot(
+            joined[other, :, pl.ds(0, block)],
+            w_other[pl.ds(0, block), lanes],
+            preferred_element_type=jnp.float32,
+        )
+
+    tiles(other_row_part)
+
+    def back_wait(source_head):
+        for slot in range(per):
+            mine = (head * per + slot == s) & (head == source_head)
+
+            @pl.when(jnp.logical_not(mine))
+            def _():
+                @pl.loop(0, CHUNKS)
+                def _(j):
+                    remote(
+                        o_out.at[0, pl.ds(j * cw, cw)],
+                        joined.at[source_head, pl.ds(slot * cols + j * cw, cw), feats],
+                        back_send.at[j, 0], back_recv.at[source_head * per + slot, j],
+                        me, other,
+                    ).wait_recv()
+
+    back_wait(head)
+    back_wait(other)
+    w_from_sibling(PIECES // 2, PIECES)
+
+    def leave(c):
+        lanes = pl.ds(pl.multiple_of(c * step, step), step)
+        return pltpu.make_async_copy(staged.at[:, lanes], out_hbm.at[:, lanes], out_sem.at[c])
+
+    @pl.loop(0, count)
+    def _(c):
+        lanes = pl.ds(pl.multiple_of(c * step, step), step)
+        total = summed[:, lanes] + jnp.dot(
+            joined[head, :, feats], w_own[feats, lanes], preferred_element_type=jnp.float32
+        )
+        total += jnp.dot(
+            joined[other, :, feats], w_other[feats, lanes], preferred_element_type=jnp.float32
+        )
+        staged[:, lanes] = total.astype(jnp.bfloat16)
+        leave(c).start()
+
+    @pl.loop(0, CHUNKS)
+    def _(j):
+        for t in range(3):
+            for d in (1, 2, 3):
+                lay(t, j, d, False).wait_send()
+        for layer in routes:
+
+            @pl.when(z == layer)
+            def _():
+                for kind, t, to, base in routes[layer]:
+                    for d in range(4):
+                        up(kind, t, j, d, to, base).wait_send()
+
+        @pl.when(z == 1)
+        def _():
+            for kind, rows, layer in ((0, LAYER, 2), (1, 2 * LAYER, 3)):
+                partial(kind, 0, j, rows, layer, 0).wait_send()
+                partial_stats(kind, 0, j, layer).wait_send()
+
+        @pl.when(z == 2)
+        def _():
+            partial(0, 1, j, LAYER, 3, LAYER).wait_send()
+            partial_stats(0, 1, j, 3).wait_send()
+
+        for d in (1, 2, 3):
+            back(j, d).wait_send()
+
+        @pl.when(jnp.logical_not(stays))
+        def _():
+            back(j, 0).wait_send()
+
+    @pl.loop(0, PIECES)
+    def _(k):
+        for q in (0, 1):
+            w_first(q, k).wait_send()
+            w_here(q, k).wait_send()
+            w_side(q, k).wait_send()
+            w_beside(q, k).wait_send()
+
+    row_copy.wait_send()
+
+    @pl.loop(0, count)
+    def _(c):
+        leave(c).wait()
+
+
+def call_layered(n, queries, keys, values, w_out, half):
+    _, stride, local_feat = queries.shape
+    depth, width = w_out.shape
+    block = local_feat // 2
+    cols = stride // LAYER
+    bf16, f32 = jnp.bfloat16, jnp.float32
+    dma = pltpu.SemaphoreType.DMA
+    blocks = cols // WIDTH
+    return pl.pallas_call(
+        functools.partial(layered, n),
+        out_shape=jax.ShapeDtypeStruct((half, width), bf16),
+        in_specs=[pl.BlockSpec(memory_space=pltpu.HBM)] * 4,
+        out_specs=pl.BlockSpec(memory_space=pltpu.HBM),
+        scratch_shapes=[pltpu.VMEM((stride, block), bf16)] * 3
+        + [
+            pltpu.VMEM((3 * LAYER, cols, block), bf16),
+            pltpu.VMEM((2 * LAYER, cols, block), bf16),
+            pltpu.VMEM((2 * LAYER, cols, block), bf16),
+            pltpu.VMEM((3 * LAYER, cols, block), bf16),
+            pltpu.VMEM((2 * LAYER, cols, block), bf16),
+            pltpu.VMEM((blocks, 8, HD), f32),
+            pltpu.VMEM((2, blocks, 8, HD), f32),
+            pltpu.VMEM((stride, block), bf16),
+            pltpu.VMEM((2, half, local_feat), bf16),
+            pltpu.VMEM((half, width), f32),
+            pltpu.VMEM((depth, width), bf16),
+            pltpu.VMEM((depth, width), bf16),
+            pltpu.VMEM((half, width), bf16),
+            dma((7,)),
+            dma((3 * CHUNKS, LAYER)),
+            dma((3 * CHUNKS, LAYER)),
+            dma((4 * CHUNKS, LAYER)),
+            dma((4 * CHUNKS, LAYER)),
+            dma((2, CHUNKS)),
+            dma((2, CHUNKS)),
+            dma((2, CHUNKS)),
+            dma((2, CHUNKS)),
+            dma((CHUNKS, LAYER)),
+            dma((2 * (half // cols), CHUNKS)),
+            dma((3, 8 * PIECES)),
+            dma((8 * PIECES,)),
+            dma,
+            dma,
+            dma((width // 512,)),
+        ],
+        compiler_params=pltpu.CompilerParams(has_side_effects=True, vmem_limit_bytes=60 * 2**20),
+    )(queries, keys, values, w_out)
 
 
 def body(
@@ -49,7 +669,7 @@
     member = lax.rem(me, 4)
     sibling = me + 1 - 2 * lax.rem(me, 2)
     beside = me + 2 - 4 * lax.div(member, 2)
-    piece = depth // (4 * PIECES)
+    piece = depth // (4 * SHARES)
 
     def col_copy(t, part, d):
         peer = lax.rem(me + d, n)
@@ -87,7 +707,7 @@
         )
 
     def index_of(who, s):
-        return who * PIECES + s
+        return who * SHARES + s
 
     member_sibling = lax.rem(sibling, 4)
     member_beside = lax.rem(beside, 4)
@@ -100,11 +720,11 @@
             for t in range(3):
                 col_copy(t, part, d).start()
 
-    @pl.loop(0, PIECES)
+    @pl.loop(0, SHARES)
     def _(s):
         w_copy(w_hbm, index_of(member, s), 0, me, other).start()
 
-    @pl.loop(PIECES - STRAIGHT, PIECES)
+    @pl.loop(SHARES - STRAIGHT, SHARES)
     def _(s):
         w_copy(w_hbm, index_of(member_beside, s), 0, me, other).start()
 
@@ -159,13 +779,13 @@
             index = index_of(member, s)
             w_copy(w_hbm, index, 0, me, other).wait_recv()
 
-            @pl.when(s < PIECES - STRAIGHT)
+            @pl.when(s < SHARES - STRAIGHT)
             def _():
                 w_copy(w_other, index, 1, beside, head).start()
 
             w_copy(w_other, index, 2, sibling, head).start()
 
-    onward(0, PIECES // 2)
+    onward(0, SHARES // 2)
 
     for copy in local[3:]:
         copy.wait()
@@ -252,9 +872,9 @@
             back_copy(part, me).start()
 
         if part == 0:
-            onward(PIECES // 2, PIECES)
-
-    @pl.loop(0, PIECES)
+            onward(SHARES // 2, SHARES)
+
+    @pl.loop(0, SHARES)
     def _(s):
         index = index_of(member_beside, s)
         w_copy(w_other, index, 1, beside, head).wait_recv()
@@ -283,7 +903,7 @@
 
     tiles(own_col_part)
 
-    @pl.loop(0, PIECES)
+    @pl.loop(0, SHARES)
     def _(s):
         w_copy(w_other, index_of(member_sibling, s), 2, sibling, head).wait_recv()
         w_copy(w_other, index_of(member_far, s), 3, sibling, head).wait_recv()
@@ -305,17 +925,17 @@
             for t in range(3):
                 col_copy(t, part, d).wait_send()
 
-    @pl.loop(0, PIECES)
+    @pl.loop(0, SHARES)
     def _(s):
         w_copy(w_hbm, index_of(member, s), 0, me, other).wait_send()
         w_copy(w_other, index_of(member, s), 2, sibling, head).wait_send()
         w_copy(w_other, index_of(member_beside, s), 3, sibling, head).wait_send()
 
-    @pl.loop(0, PIECES - STRAIGHT)
+    @pl.loop(0, SHARES - STRAIGHT)
     def _(s):
         w_copy(w_other, index_of(member, s), 1, beside, head).wait_send()
 
-    @pl.loop(PIECES - STRAIGHT, PIECES)
+    @pl.loop(SHARES - STRAIGHT, SHARES)
     def _(s):
         w_copy(w_hbm, index_of(member_beside, s), 0, me, other).wait_send()
 
@@ -339,6 +959,9 @@
     assert queries.shape[0] == 1 and local_feat == 2 * block
     half = stride // lax.axis_size("head")
     cols = stride // n
+    if n == LAYER * LAYER and stride % (LAYER * CHUNKS * WIDTH) == 0:
+        out = call_layered(n, queries, keys, values, w_out, half)
+        return out.reshape((1, half, model_width))
     bf16 = jnp.bfloat16
     dma = pltpu.SemaphoreType.DMA
     out = pl.pallas_call(
@@ -359,8 +982,8 @@
             dma((3 * PARTS, n)),
             dma((PARTS, n)),
             dma((2 * PARTS, n // 2)),
-            dma((4, 4 * PIECES)),
-            dma((4 * PIECES,)),
+            dma((4, 4 * SHARES)),
+            dma((4 * SHARES,)),
             dma,
             dma,
         ],

time: 121 us -> 113 us (0.934); the launches traced: 119 us -> 112 us
  Pallas kernels: 114 us -> 108 us
    pallas_call x1, Pallas kernels: 114 us -> 108 us  [call_layered(): pl.pallas_call(functools.partial(layered, n), out_shape=jax.ShapeDtypeStr...]
where the time goes in v1:
time: 113 us; the launch traced here: 112 us
  Pallas kernels  108 us (96%)
  local copies, waits for them, and re-layouts  4.7 us (4%)
    pallas_call x1, Pallas kernels, call_layered(): pl.pallas_call(functools.partial(layered, n), out_shape=jax.ShapeDtypeStr...  108 us
    unnamed x1, local copies, waits for them, and re-layouts  4.7 us

profile of v1, /device:TPU:25, one launch (start us, length us, event | category | flops | bytes accessed | tf_op | source)
XLA Modules:
  0.0 112.2 jit_solution(17874980939485776462)
XLA Ops:
  0.0 107.5 %shard_map.46 = bf16[512,4096]{1,0:T(8,128)(2,1)} custom-call(bf16[1,1024,1024]{2,1,0:T(8,128)(2,1)} %q_hbm.1, bf16[1,1024,1024]{2,1,0:T(8,128)(2,1)} %k_hbm.1, bf16[1,1024,1024]{2,1,0:T(8,128)(2,1)} %v_hbm.1, bf16[1024,4096]{1,0:T(8,128)(2,1)} %w_hbm.1), custom_call_target="tpu_custom_call" | custom-call | tf_op jit(solution)/shard_map/pallas_call | solution.py:611
  107.5 4.7 %copy.6 = bf16[1,512,4096]{2,1,0:T(8,128)(2,1)} copy(bf16[1,512,4096]{2,1,0:T(8,128)(2,1)} %bitcast.1) | data formatting | bytes 8388608

commit v2 on v1

--- a/solution.py
+++ b/solution.py
@@ -16,8 +16,9 @@
 LAYER = 4
 CHUNKS = 8
 WIDTH = 16
+WIDTH_LOG = 4
 PIECES = 4
-AHEAD = 2
+AHEAD = 3
 
 masked_score = -1e30
 
@@ -236,40 +237,41 @@
             key_index[:, :end] <= row_index[:, :end] + start,
         )
 
-    def spread(sums, size, off):
+    def spread(sums):
+        lane = lax.broadcasted_iota(jnp.int32, (HD, HD), 1)
+        row = lax.broadcasted_iota(jnp.int32, (HD, HD), 0)
+        return jnp.sum(jnp.where(lane == row, sums, 0.0), axis=0, keepdims=True)
+
+    def column(line, off, period):
         lane = lax.broadcasted_iota(jnp.int32, (size, HD), 1)
         row = lax.broadcasted_iota(jnp.int32, (size, HD), 0)
-        return jnp.sum(jnp.where(lane == row + off, sums, 0.0), axis=0, keepdims=True)
-
-    def column(line, size, off):
-        lane = lax.broadcasted_iota(jnp.int32, (size, HD), 1)
-        row = lax.broadcasted_iota(jnp.int32, (size, HD), 0)
-        return jnp.sum(jnp.where(lane == row + off, line, 0.0), axis=1, keepdims=True)
+        at = off + (row & (WIDTH - 1)) + lax.shift_right_logical(row, WIDTH_LOG) * period
+        return jnp.sum(jnp.where(lane == at, line, 0.0), axis=1, keepdims=True)
 
     heads = block // HD
     size = LAYER * WIDTH
 
-    def small(q_at, q_rows, k_at, k_rows, c, b, causal, keep):
-        start = pl.multiple_of(c * cw + b * WIDTH, WIDTH)
-        shape = (q_rows * WIDTH, k_rows * WIDTH)
+    def small(q_at, q_rows, k_at, k_rows, c, b, width, causal, keep):
+        start = pl.multiple_of(c * cw + b * width, width)
+        shape = (q_rows * width, k_rows * width)
         r = lax.broadcasted_iota(jnp.int32, shape, 0)
         m = lax.broadcasted_iota(jnp.int32, shape, 1)
-        allowed = ((r - m) & (WIDTH - 1)) == 0
+        allowed = ((r - m) & (width - 1)) == 0
         if causal is not None:
-            allowed &= m <= r + causal * WIDTH
+            allowed &= m <= r + causal * width
         for h in range(heads):
             lanes = pl.ds(h * HD, HD)
-            q_slice = (pl.ds(q_at, q_rows), pl.ds(start, WIDTH), lanes)
-            k_slice = (pl.ds(k_at, k_rows), pl.ds(start, WIDTH), lanes)
+            q_slice = (pl.ds(q_at, q_rows), pl.ds(start, width), lanes)
+            k_slice = (pl.ds(k_at, k_rows), pl.ds(start, width), lanes)
             got, sums = weigh(
                 q_in[q_slice].reshape(shape[0], HD),
                 k_in[k_slice].reshape(shape[1], HD),
                 v_in[k_slice].reshape(shape[1], HD),
                 allowed,
             )
-            o_out[q_slice] = got.reshape(q_rows, WIDTH, HD)
-            if keep is not None:
-                stats[c * (cw // WIDTH) + b, pl.ds(h, 1)] = spread(sums, shape[0], keep)
+            o_out[q_slice] = got.reshape(q_rows, width, HD)
+            if keep:
+                stats[c * strips + b, pl.ds(h, 1)] = spread(sums)
 
     strips = cw // WIDTH
 
@@ -318,7 +320,7 @@
             for d in range(4):
                 up_arrival(kind, t, j, d, base).wait_recv()
         for b in range(strips):
-            small(LAYER, 2 * LAYER, 0, 2 * LAYER, j, b, None, 0)
+            small(LAYER, 2 * LAYER, 0, 2 * LAYER, j, b, WIDTH, None, True)
         for kind, rows, layer in ((0, LAYER, 2), (1, 2 * LAYER, 3)):
             partial(kind, 0, j, rows, layer, 0).start()
             partial_stats(kind, 0, j, layer).start()
@@ -329,16 +331,14 @@
             for t, ds in ((0, (1, 2, 3)), (1, (1,)), (2, (1,))):
                 for d in ds:
                     lay(t, c, d, True).wait_recv()
-            for b in range(strips):
-                small(0, LAYER, LAYER, LAYER, c, b, 0, None)
+            small(0, LAYER, LAYER, LAYER, c, 0, cw, 0, False)
             back_all(c)
 
         @pl.when(z == 1)
         def _():
             for d in (1, 2, 3):
                 lay(0, c, d, True).wait_recv()
-            for b in range(strips):
-                small(0, LAYER, 0, 2 * LAYER, c, b, LAYER, None)
+            small(0, LAYER, 0, 2 * LAYER, c, 0, cw, LAYER, False)
             back_all(c)
 
         @pl.when(z >= 2)
@@ -353,36 +353,29 @@
             for d in range(4):
                 up_arrival(2, 0, c, d, LAYER).wait_recv()
             for b in range(strips):
-                small(0, 2 * LAYER, LAYER, LAYER, c, b, 0, 0)
+                small(0, 2 * LAYER, LAYER, LAYER, c, b, WIDTH, 0, True)
             partial(0, 1, c, LAYER, 3, LAYER).start()
             partial_stats(0, 1, c, 3).start()
 
         @pl.when(z == 3)
         def _():
-            for b in range(strips):
-                small(0, LAYER, LAYER, LAYER, c, b, 0, size)
+            small(0, LAYER, LAYER, LAYER, c, 0, cw, 0, True)
 
     def combine(c):
-        def weights(lines):
-            top = functools.reduce(jnp.maximum, lines)
-            terms = [jnp.exp(line - top) for line in lines]
-            total = functools.reduce(jnp.add, terms)
-            return [term / total for term in terms]
-
-        def mix(b, lines, off):
+        def mix(b, parts):
             start = pl.multiple_of(c * cw + b * WIDTH, WIDTH)
-            shares = weights(lines)
+            rows = pl.ds(start, WIDTH)
             for h in range(heads):
                 lanes = pl.ds(h * HD, HD)
-                at = (pl.ds(0, LAYER), pl.ds(start, WIDTH), lanes)
-                parts = [o_out[at], p_in[at]]
-                if len(lines) == 3:
-                    parts.append(p_in[pl.ds(LAYER, LAYER), pl.ds(start, WIDTH), lanes])
-                total = 0.0
-                for part, share in zip(parts, shares):
-                    weight = column(share[h : h + 1], size, off)
-                    total += part.reshape(size, HD).astype(jnp.float32) * weight
-                o_out[at] = total.astype(jnp.bfloat16).reshape(LAYER, WIDTH, HD)
+                lines = [column(ref[strip, pl.ds(h, 1)], off, period) for _, _, ref, strip, off, period in parts]
+                top = functools.reduce(jnp.maximum, lines)
+                terms = [jnp.exp(line - top) for line in lines]
+                total = functools.reduce(jnp.add, terms)
+                got = 0.0
+                for (source, base, *_), term in zip(parts, terms):
+                    value = source[pl.ds(base, LAYER), rows, lanes].reshape(size, HD)
+                    got += value.astype(jnp.float32) * (term / total)
+                o_out[pl.ds(0, LAYER), rows, lanes] = got.astype(jnp.bfloat16).reshape(LAYER, WIDTH, HD)
 
         def wait(slot):
             partial(0, slot, c, 0, 0, slot * LAYER).wait_recv()
@@ -393,7 +386,13 @@
             wait(0)
             for b in range(strips):
                 strip = c * strips + b
-                mix(b, [stats[strip, :heads], stats_in[0, strip, :heads]], 0)
+                mix(
+                    b,
+                    [
+                        (o_out, 0, stats, strip, 0, WIDTH),
+                        (p_in, 0, stats_in.at[0], strip, 0, WIDTH),
+                    ],
+                )
             back_all(c)
 
         @pl.when(z == 3)
@@ -404,56 +403,83 @@
                 strip = c * strips + b
                 mix(
                     b,
-                    [stats[strip, :heads], stats_in[0, strip, :heads], stats_in[1, strip, :heads]],
-                    size,
+                    [
+                        (o_out, 0, stats, c * strips, b * WIDTH, cw),
+                        (p_in, 0, stats_in.at[0], strip, size, WIDTH),
+                        (p_in, LAYER, stats_in.at[1], strip, size, WIDTH),
+                    ],
                 )
             back_all(c)
-
-    def step_of(h, u):
-        j = 2 * h + u
-        tiles_of = [start for i, start in enumerate(range(0, stride, tile)) if (i % 4 in (0, 3)) == (u == 0)]
-        for start in tiles_of:
-            row_tile(h, start)
-        for layer in routes:
-
-            @pl.when(z == layer)
-            def _():
-                relay(layer, j)
-
-                @pl.when(j + AHEAD < CHUNKS)
-                def _():
-                    direct(layer, j + AHEAD)
-
-        @pl.when(z == 1)
-        def _():
-            ext(j)
-
-        if u == 0:
-
-            @pl.when(h > 0)
-            def _():
-                w_in(1, h - 1)
-
-        else:
-            w_in(0, h)
-
-        @pl.when(h >= heads // 2)
-        def _():
-            c = 4 * (h - heads // 2) + 2 * u
-            own(c)
-            own(c + 1)
-
-    @pl.loop(0, heads)
-    def _(h):
-        step_of(h, 0)
-        step_of(h, 1)
 
     row_copy = remote(
         row_out.at[pl.ds(pl.multiple_of(other * half, half), half)],
         joined.at[head, :, pl.ds(0, block)], row_send, row_recv, me, other,
     )
-    row_copy.start()
-    joined[head, :, pl.ds(0, block)] = row_out[pl.ds(pl.multiple_of(head * half, half), half)]
+    step = 512
+    count = staged.shape[1] // step
+
+    def tiles(add):
+        @pl.loop(0, count)
+        def _(c):
+            add(pl.ds(pl.multiple_of(c * step, step), step))
+
+    def own_row_part(lanes):
+        summed[:, lanes] = jnp.dot(
+            joined[head, :, pl.ds(0, block)],
+            w_own[pl.ds(0, block), lanes],
+            preferred_element_type=jnp.float32,
+        )
+
+    @pl.loop(0, CHUNKS)
+    def _(j):
+        @pl.when(j < 2)
+        def _():
+            @pl.loop(j * (heads // 2), (j + 1) * (heads // 2))
+            def _(h):
+                for start in range(0, stride, tile):
+                    row_tile(h, start)
+
+        @pl.when(j == 1)
+        def _():
+            row_copy.start()
+            joined[head, :, pl.ds(0, block)] = row_out[pl.ds(pl.multiple_of(head * half, half), half)]
+
+        for layer in routes:
+
+            @pl.when(z == layer)
+            def _():
+                relay(layer, j)
+
+                @pl.when(j + AHEAD < CHUNKS)
+                def _():
+                    direct(layer, j + AHEAD)
+
+        @pl.when(z == 1)
+        def _():
+            ext(j)
+
+        @pl.when(j == 2)
+        def _():
+            local[6].wait()
+            tiles(own_row_part)
+
+        @pl.when((j > 0) & (lax.rem(j, 2) == 1))
+        def _():
+            w_in(0, lax.div(j, 2))
+
+        @pl.when((j > 0) & (lax.rem(j, 2) == 0))
+        def _():
+            w_in(1, lax.div(j, 2) - 1)
+
+        @pl.when(j >= CHUNKS // 2)
+        def _():
+            c = 2 * j - CHUNKS
+            own(c)
+            own(c + 1)
+
+            @pl.when(z >= 2)
+            def _():
+                combine(j - CHUNKS // 2)
 
     w_in(1, PIECES - 1)
 
@@ -463,27 +489,9 @@
         def _(k):
             w_side(1, k).start()
 
-    local[6].wait()
-    step = 512
-    count = staged.shape[1] // step
-
-    def tiles(add):
-        @pl.loop(0, count)
-        def _(c):
-            add(pl.ds(pl.multiple_of(c * step, step), step))
-
-    def own_row_part(lanes):
-        summed[:, lanes] = jnp.dot(
-            joined[head, :, pl.ds(0, block)],
-            w_own[pl.ds(0, block), lanes],
-            preferred_element_type=jnp.float32,
-        )
-
-    tiles(own_row_part)
-
     @pl.when(z >= 2)
     def _():
-        @pl.loop(0, CHUNKS - 2)
+        @pl.loop(CHUNKS // 2, CHUNKS - 2)
         def _(c):
             combine(c)
 
@@ -497,17 +505,17 @@
         def _(c):
             combine(c)
 
-    @pl.loop(0, PIECES)
+    @pl.loop(0, PIECES // 2)
     def _(k):
         w_on(1, k)
 
-    def w_from_sibling(first, last):
+    def w_from_sibling(qs, first, last):
         @pl.loop(first, last)
         def _(k):
-            for q in range(4):
+            for q in qs:
                 w_copy(w_other, q, 1 - core, k, 1, here(sib), head).wait_recv()
 
-    w_from_sibling(0, PIECES // 2)
+    w_from_sibling((0, 1, 2, 3), 0, PIECES // 2)
     row_copy.wait_recv()
 
     def other_row_part(lanes):
@@ -536,7 +544,26 @@
 
     back_wait(head)
     back_wait(other)
-    w_from_sibling(PIECES // 2, PIECES)
+    w_from_sibling((2 * even, 2 * even + 1), PIECES // 2, PIECES)
+    quarter = block // 2
+    early = pl.ds(pl.multiple_of(block + even * quarter, quarter), quarter)
+    late = pl.ds(pl.multiple_of(block + (1 - even) * quarter, quarter), quarter)
+
+    def col_part(lanes):
+        total = summed[:, lanes] + jnp.dot(
+            joined[head, :, feats], w_own[feats, lanes], preferred_element_type=jnp.float32
+        )
+        summed[:, lanes] = total + jnp.dot(
+            joined[other, :, early], w_other[early, lanes], preferred_element_type=jnp.float32
+        )
+
+    tiles(col_part)
+
+    @pl.loop(PIECES // 2, PIECES)
+    def _(k):
+        w_on(1, k)
+
+    w_from_sibling((2 - 2 * even, 3 - 2 * even), PIECES // 2, PIECES)
 
     def leave(c):
         lanes = pl.ds(pl.multiple_of(c * step, step), step)
@@ -546,10 +573,7 @@
     def _(c):
         lanes = pl.ds(pl.multiple_of(c * step, step), step)
         total = summed[:, lanes] + jnp.dot(
-            joined[head, :, feats], w_own[feats, lanes], preferred_element_type=jnp.float32
-        )
-        total += jnp.dot(
-            joined[other, :, feats], w_other[feats, lanes], preferred_element_type=jnp.float32
+            joined[other, :, late], w_other[late, lanes], preferred_element_type=jnp.float32
         )
         staged[:, lanes] = total.astype(jnp.bfloat16)
         leave(c).start()

time: 113 us -> 115 us (1.018)
    pallas_call x1, Pallas kernels: 108 us -> 109 us  [call_layered(): pl.pallas_call(functools.partial(layered, n), out_shape=jax.ShapeDtypeStr...]
where the time goes in v2:
time: 115 us; the launch traced here: 114 us
  Pallas kernels  109 us (95%)
  local copies, waits for them, and re-layouts  4.7 us (4%)
    pallas_call x1, Pallas kernels, call_layered(): pl.pallas_call(functools.partial(layered, n), out_shape=jax.ShapeDtypeStr...  109 us
    unnamed x1, local copies, waits for them, and re-layouts  4.7 us

profile of v2, /device:TPU:25, one launch (start us, length us, event | category | flops | bytes accessed | tf_op | source)
XLA Modules:
  0.0 113.7 jit_solution(7532333478202351794)
XLA Ops:
  0.0 109.0 %shard_map.46 = bf16[512,4096]{1,0:T(8,128)(2,1)} custom-call(bf16[1,1024,1024]{2,1,0:T(8,128)(2,1)} %q_hbm.1, bf16[1,1024,1024]{2,1,0:T(8,128)(2,1)} %k_hbm.1, bf16[1,1024,1024]{2,1,0:T(8,128)(2,1)} %v_hbm.1, bf16[1024,4096]{1,0:T(8,128)(2,1)} %w_hbm.1), custom_call_target="tpu_custom_call" | custom-call | tf_op jit(solution)/shard_map/pallas_call | solution.py:635
  109.0 4.7 %copy.6 = bf16[1,512,4096]{2,1,0:T(8,128)(2,1)} copy(bf16[1,512,4096]{2,1,0:T(8,128)(2,1)} %bitcast.1) | data formatting | bytes 8388608

commit v3 on v2

--- a/solution.py
+++ b/solution.py
@@ -35,23 +35,29 @@
     return (mixed / total).astype(jnp.bfloat16)
 
 
-def weigh(query, key, value, allowed):
-    scores = lax.dot_general(
-        query, key, (((1,), (1,)), ((), ())), preferred_element_type=jnp.float32
-    ) * jnp.float32(1.0 / HD**0.5)
-    if allowed is not None:
-        scores = jnp.where(allowed, scores, masked_score)
-    top = jnp.max(scores, axis=-1, keepdims=True)
-    expo = jnp.exp(scores - top)
-    total = jnp.sum(expo, axis=-1, keepdims=True)
-    mixed = jnp.dot(expo.astype(jnp.bfloat16), value, preferred_element_type=jnp.float32)
-    return (mixed / total).astype(jnp.bfloat16), top + jnp.log(total)
+def weigh(queries, keys, values, allowed):
+    scores = [
+        lax.dot_general(q, k, (((1,), (1,)), ((), ())), preferred_element_type=jnp.float32)
+        for q, k in zip(queries, keys)
+    ]
+    scores = [jnp.where(allowed, s * jnp.float32(1.0 / HD**0.5), masked_score) for s in scores]
+    tops = [jnp.max(s, axis=-1, keepdims=True) for s in scores]
+    expos = [jnp.exp(s - top) for s, top in zip(scores, tops)]
+    totals = [jnp.sum(e, axis=-1, keepdims=True) for e in expos]
+    mixed = [
+        jnp.dot(e.astype(jnp.bfloat16), v, preferred_element_type=jnp.float32)
+        for e, v in zip(expos, values)
+    ]
+    return [
+        ((m / total).astype(jnp.bfloat16), top + jnp.log(total))
+        for m, total, top in zip(mixed, totals, tops)
+    ]
 
 
 def layered(
     n, q_hbm, k_hbm, v_hbm, w_hbm, out_hbm, q_row, k_row, v_row, q_in, k_in, v_in, o_out, p_in,
     stats, stats_in, row_out, joined, summed, w_own, w_other, staged,
-    local_sem, lay_send, lay_recv, up_send, up_recv, part_send, part_recv, stat_send, stat_recv,
+    local_sem, chunk_sem, lay_send, lay_recv, up_send, up_recv, part_send, part_recv,
     back_send, back_recv, w_send, w_recv, row_send, row_recv, out_sem,
 ):
     me, head = lax.axis_index("ctx"), lax.axis_index("head")
@@ -68,14 +74,16 @@
     half = joined.shape[1]
     cols = stride // LAYER
     cw = cols // CHUNKS
-    per = half // cols
     hbm = (q_hbm, k_hbm, v_hbm)
     ins = (q_in, k_in, v_in)
     own_at = (0, LAYER, LAYER)
-    back_head = lax.div(s * cols, half)
-    back_start = lax.rem(s * cols, half)
-    stays = back_head == head
     feats = pl.ds(block, block)
+
+    def place(j, slot):
+        return slot * (cols // 2) + lax.div(j, 2) * cw
+
+    def chunk_of(j, slot):
+        return pl.ds(pl.multiple_of(lax.rem(j, 2) * half + place(j, slot), cw), cw)
 
     def remote(src, dst, send, recv, ctx, at):
         return pltpu.make_async_remote_copy(
@@ -89,7 +97,7 @@
     def lay(t, j, d, source):
         row = peers[d] if source else s
         return remote(
-            hbm[t].at[0, pl.ds(peers[d] * cols + j * cw, cw), feats],
+            hbm[t].at[0, chunk_of(j, peers[d]), feats],
             ins[t].at[own_at[t] + row, pl.ds(j * cw, cw)],
             lay_send.at[t * CHUNKS + j, d], lay_recv.at[t * CHUNKS + j, d],
             here(peers[d]), head,
@@ -97,7 +105,7 @@
 
     def up(kind, t, j, d, layer, base):
         if d < 2:
-            src, slot, row = hbm[t].at[0, pl.ds(peers[d] * cols + j * cw, cw), feats], peers[d], s
+            src, slot, row = hbm[t].at[0, chunk_of(j, peers[d]), feats], peers[d], s
         else:
             src, slot, row = ins[t].at[own_at[t] + peers[d], pl.ds(j * cw, cw)], s, peers[d]
         return remote(
@@ -116,8 +124,20 @@
     routes = {
         0: ((0, 1, 1, 0), (1, 2, 1, 0)),
         2: ((2, 0, 1, LAYER),),
-        3: ((3, 0, 1, 2 * LAYER), (2, 0, 2, LAYER)),
+        3: ((2, 0, 2, LAYER),),
     }
+
+    def onward(j):
+        at = pl.ds(j * cw, cw)
+        return remote(
+            q_in.at[pl.ds(LAYER, LAYER), at], q_in.at[pl.ds(2 * LAYER, LAYER), at],
+            up_send.at[3 * CHUNKS + j, 0], up_recv.at[3 * CHUNKS + j, 0], LAYER + s, head,
+        )
+
+    def pass_on(j):
+        for d in range(4):
+            up_arrival(2, 0, j, d, LAYER).wait_recv()
+        onward(j).start()
 
     def direct(layer, j):
         for kind, t, to, base in routes[layer]:
@@ -170,7 +190,7 @@
             w_side(q, k).start()
         else:
 
-            @pl.when(z_early)
+            @pl.when(z_early | (k > 0))
             def _():
                 w_side(q, k).start()
 
@@ -213,14 +233,17 @@
     ]
     local += [
         pltpu.make_async_copy(
-            hbm[t].at[0, pl.ds(s * cols, cols), feats], ins[t].at[own_at[t] + s], local_sem.at[3 + t]
+            hbm[t].at[0, chunk_of(j, s), feats],
+            ins[t].at[own_at[t] + s, pl.ds(j * cw, cw)],
+            chunk_sem.at[t, j],
         )
         for t in range(3)
+        for j in range(CHUNKS)
     ]
-    local.append(pltpu.make_async_copy(w_hbm, w_own, local_sem.at[6]))
+    local.append(pltpu.make_async_copy(w_hbm, w_own, local_sem.at[3]))
     for copy in local:
         copy.start()
-    for copy in local[:6]:
+    for copy in local[:-1]:
         copy.wait()
 
     tile = min(256, half)
@@ -242,6 +265,11 @@
         row = lax.broadcasted_iota(jnp.int32, (HD, HD), 0)
         return jnp.sum(jnp.where(lane == row, sums, 0.0), axis=0, keepdims=True)
 
+    def laid(sums, off):
+        lane = lax.broadcasted_iota(jnp.int32, (size, HD), 1)
+        row = lax.broadcasted_iota(jnp.int32, (size, HD), 0)
+        return jnp.sum(jnp.where(lane == row + off, sums, 0.0), axis=0, keepdims=True)
+
     def column(line, off, period):
         lane = lax.broadcasted_iota(jnp.int32, (size, HD), 1)
         row = lax.broadcasted_iota(jnp.int32, (size, HD), 0)
@@ -259,71 +287,77 @@
         allowed = ((r - m) & (width - 1)) == 0
         if causal is not None:
             allowed &= m <= r + causal * width
+        slices = []
         for h in range(heads):
             lanes = pl.ds(h * HD, HD)
-            q_slice = (pl.ds(q_at, q_rows), pl.ds(start, width), lanes)
-            k_slice = (pl.ds(k_at, k_rows), pl.ds(start, width), lanes)
-            got, sums = weigh(
-                q_in[q_slice].reshape(shape[0], HD),
-                k_in[k_slice].reshape(shape[1], HD),
-                v_in[k_slice].reshape(shape[1], HD),
-                allowed,
+            slices.append(
+                (
+                    (pl.ds(q_at, q_rows), pl.ds(start, width), lanes),
+                    (pl.ds(k_at, k_rows), pl.ds(start, width), lanes),
+                )
             )
-            o_out[q_slice] = got.reshape(q_rows, width, HD)
+        found = weigh(
+            [q_in[at].reshape(shape[0], HD) for at, _ in slices],
+            [k_in[at].reshape(shape[1], HD) for _, at in slices],
+            [v_in[at].reshape(shape[1], HD) for _, at in slices],
+            allowed,
+        )
+        for h, (got, sums) in enumerate(found):
+            o_out[slices[h][0]] = got.reshape(q_rows, width, HD)
             if keep:
                 stats[c * strips + b, pl.ds(h, 1)] = spread(sums)
 
     strips = cw // WIDTH
 
-    def partial(kind, slot, j, rows, layer, base):
+    def partial(j, rows, layer):
         return remote(
-            o_out.at[pl.ds(rows, LAYER), pl.ds(j * cw, cw)],
-            p_in.at[pl.ds(base, LAYER), pl.ds(j * cw, cw)],
-            part_send.at[kind, j], part_recv.at[slot, j], layer * LAYER + s, head,
-        )
-
-    def partial_stats(kind, slot, j, layer):
+            o_out.at[pl.ds(LAYER, rows), pl.ds(j * cw, cw)], p_in.at[pl.ds(0, rows), pl.ds(j * cw, cw)],
+            part_send.at[0, j], part_recv.at[0, j], layer * LAYER + s, head,
+        )
+
+    def partial_stats(j, layer):
         at = pl.ds(j * strips, strips)
         return remote(
-            stats.at[at], stats_in.at[slot, at],
-            stat_send.at[kind, j], stat_recv.at[slot, j], layer * LAYER + s, head,
+            stats.at[at], stats_in.at[at], part_send.at[1, j], part_recv.at[1, j], layer * LAYER + s, head
         )
 
     def back(j, d):
-        row = peers[d]
         return remote(
-            o_out.at[row, pl.ds(j * cw, cw)],
-            joined.at[head, pl.ds(back_start + j * cw, cw), feats],
-            back_send.at[j, d], back_recv.at[head * per + lax.rem(s, per), j],
-            here(row), back_head,
-        )
+            o_out.at[peers[d], pl.ds(j * cw, cw)],
+            joined.at[head, pl.ds(place(j, s), cw), feats],
+            back_send.at[j, d], back_recv.at[head * LAYER + s, lax.div(j, 2)],
+            here(peers[d]), lax.rem(j, 2),
+        )
+
+    def stays(j):
+        return lax.rem(j, 2) == head
 
     def back_all(j):
         for d in (2, 3, 1):
             back(j, d).start()
 
-        @pl.when(jnp.logical_not(stays))
+        @pl.when(jnp.logical_not(stays(j)))
         def _():
             back(j, 0).start()
 
-        @pl.when(stays)
-        def _():
-            joined[head, pl.ds(pl.multiple_of(back_start + j * cw, WIDTH), cw), feats] = o_out[
-                s, pl.ds(pl.multiple_of(j * cw, WIDTH), cw)
+        @pl.when(stays(j))
+        def _():
+            joined[head, pl.ds(pl.multiple_of(place(j, s), cw), cw), feats] = o_out[
+                s, pl.ds(pl.multiple_of(j * cw, cw), cw)
             ]
 
     def ext(j):
         for t in (1, 2):
             for d in (1, 2, 3):
                 lay(t, j, d, True).wait_recv()
-        for kind, t, base in ((0, 1, 0), (1, 2, 0), (2, 0, LAYER), (3, 0, 2 * LAYER)):
+        for kind, t, base in ((0, 1, 0), (1, 2, 0), (2, 0, LAYER)):
             for d in range(4):
                 up_arrival(kind, t, j, d, base).wait_recv()
+        onward(j).wait_recv()
         for b in range(strips):
             small(LAYER, 2 * LAYER, 0, 2 * LAYER, j, b, WIDTH, None, True)
-        for kind, rows, layer in ((0, LAYER, 2), (1, 2 * LAYER, 3)):
-            partial(kind, 0, j, rows, layer, 0).start()
-            partial_stats(kind, 0, j, layer).start()
+        partial(j, 2 * LAYER, 2).start()
+        partial_stats(j, 2).start()
 
     def own(c):
         @pl.when(z == 0)
@@ -350,66 +384,70 @@
 
         @pl.when(z == 2)
         def _():
-            for d in range(4):
-                up_arrival(2, 0, c, d, LAYER).wait_recv()
             for b in range(strips):
                 small(0, 2 * LAYER, LAYER, LAYER, c, b, WIDTH, 0, True)
-            partial(0, 1, c, LAYER, 3, LAYER).start()
-            partial_stats(0, 1, c, 3).start()
 
         @pl.when(z == 3)
         def _():
             small(0, LAYER, LAYER, LAYER, c, 0, cw, 0, True)
 
     def combine(c):
-        def mix(b, parts):
+        def mix(b, base, parts, keep):
             start = pl.multiple_of(c * cw + b * WIDTH, WIDTH)
             rows = pl.ds(start, WIDTH)
+            strip = c * strips + b
             for h in range(heads):
                 lanes = pl.ds(h * HD, HD)
-                lines = [column(ref[strip, pl.ds(h, 1)], off, period) for _, _, ref, strip, off, period in parts]
+                lines = [column(ref[at, pl.ds(row + h, 1)], off, period) for _, _, ref, at, row, off, period in parts]
                 top = functools.reduce(jnp.maximum, lines)
                 terms = [jnp.exp(line - top) for line in lines]
                 total = functools.reduce(jnp.add, terms)
                 got = 0.0
-                for (source, base, *_), term in zip(parts, terms):
-                    value = source[pl.ds(base, LAYER), rows, lanes].reshape(size, HD)
+                for (source, first, *_), term in zip(parts, terms):
+                    value = source[pl.ds(first, LAYER), rows, lanes].reshape(size, HD)
                     got += value.astype(jnp.float32) * (term / total)
-                o_out[pl.ds(0, LAYER), rows, lanes] = got.astype(jnp.bfloat16).reshape(LAYER, WIDTH, HD)
-
-        def wait(slot):
-            partial(0, slot, c, 0, 0, slot * LAYER).wait_recv()
-            partial_stats(0, slot, c, 0).wait_recv()
+                o_out[pl.ds(base, LAYER), rows, lanes] = got.astype(jnp.bfloat16).reshape(LAYER, WIDTH, HD)
+                if keep:
+                    stats[strip, pl.ds(heads + h, 1)] = laid(top + jnp.log(total), size)
 
         @pl.when(z == 2)
         def _():
-            wait(0)
+            partial(c, 2 * LAYER, 2).wait_recv()
+            partial_stats(c, 2).wait_recv()
+            for first in (LAYER, 0):
+                off = size if first else 0
+                for b in range(strips):
+                    strip = c * strips + b
+                    mix(
+                        b,
+                        first,
+                        [
+                            (o_out, first, stats, strip, 0, off, WIDTH),
+                            (p_in, first, stats_in, strip, 0, off, WIDTH),
+                        ],
+                        first > 0,
+                    )
+                if first:
+                    partial(c, LAYER, 3).start()
+                    partial_stats(c, 3).start()
+
+        @pl.when(z == 3)
+        def _():
+            partial(c, LAYER, 3).wait_recv()
+            partial_stats(c, 3).wait_recv()
             for b in range(strips):
                 strip = c * strips + b
                 mix(
                     b,
+                    0,
                     [
-                        (o_out, 0, stats, strip, 0, WIDTH),
-                        (p_in, 0, stats_in.at[0], strip, 0, WIDTH),
+                        (o_out, 0, stats, c * strips, 0, b * WIDTH, cw),
+                        (p_in, 0, stats_in, strip, heads, size, WIDTH),
                     ],
+                    False,
                 )
-            back_all(c)
-
-        @pl.when(z == 3)
-        def _():
-            wait(0)
-            wait(1)
-            for b in range(strips):
-                strip = c * strips + b
-                mix(
-                    b,
-                    [
-                        (o_out, 0, stats, c * strips, b * WIDTH, cw),
-                        (p_in, 0, stats_in.at[0], strip, size, WIDTH),
-                        (p_in, LAYER, stats_in.at[1], strip, size, WIDTH),
-                    ],
-                )
-            back_all(c)
+
+        back_all(c)
 
     row_copy = remote(
         row_out.at[pl.ds(pl.multiple_of(other * half, half), half)],
@@ -446,13 +484,17 @@
 
         for layer in routes:
 
-            @pl.when(z == layer)
+            @pl.when((z == layer) & (j < CHUNKS // 2))
             def _():
-                relay(layer, j)
-
-                @pl.when(j + AHEAD < CHUNKS)
-                def _():
-                    direct(layer, j + AHEAD)
+                @pl.loop(2 * j, 2 * j + 2)
+                def _(c):
+                    relay(layer, c)
+                    if layer == 2:
+                        pass_on(c)
+
+                    @pl.when(c + AHEAD < CHUNKS)
+                    def _():
+                        direct(layer, c + AHEAD)
 
         @pl.when(z == 1)
         def _():
@@ -460,8 +502,12 @@
 
         @pl.when(j == 2)
         def _():
-            local[6].wait()
+            local[-1].wait()
             tiles(own_row_part)
+
+        @pl.when(jnp.logical_not(z_early) & (j == CHUNKS // 2))
+        def _():
+            w_side(1, 0).start()
 
         @pl.when((j > 0) & (lax.rem(j, 2) == 1))
         def _():
@@ -477,21 +523,15 @@
             own(c)
             own(c + 1)
 
-            @pl.when(z >= 2)
+            @pl.when((z >= 2) & (j > CHUNKS // 2))
             def _():
-                combine(j - CHUNKS // 2)
+                combine(j - CHUNKS // 2 - 1)
 
     w_in(1, PIECES - 1)
-
-    @pl.when(jnp.logical_not(z_early))
-    def _():
-        @pl.loop(0, PIECES)
-        def _(k):
-            w_side(1, k).start()
 
     @pl.when(z >= 2)
     def _():
-        @pl.loop(CHUNKS // 2, CHUNKS - 2)
+        @pl.loop(CHUNKS // 2 - 1, CHUNKS - 2)
         def _(c):
             combine(c)
 
@@ -528,17 +568,16 @@
     tiles(other_row_part)
 
     def back_wait(source_head):
-        for slot in range(per):
-            mine = (head * per + slot == s) & (head == source_head)
-
-            @pl.when(jnp.logical_not(mine))
+        for slot in range(LAYER):
+
+            @pl.when(jnp.logical_not((slot == s) & (head == source_head)))
             def _():
-                @pl.loop(0, CHUNKS)
-                def _(j):
+                @pl.loop(0, CHUNKS // 2)
+                def _(i):
                     remote(
-                        o_out.at[0, pl.ds(j * cw, cw)],
-                        joined.at[source_head, pl.ds(slot * cols + j * cw, cw), feats],
-                        back_send.at[j, 0], back_recv.at[source_head * per + slot, j],
+                        o_out.at[0, pl.ds(i * cw, cw)],
+                        joined.at[source_head, pl.ds(place(2 * i, slot), cw), feats],
+                        back_send.at[i, 0], back_recv.at[source_head * LAYER + slot, i],
                         me, other,
                     ).wait_recv()
 
@@ -593,19 +632,19 @@
 
         @pl.when(z == 1)
         def _():
-            for kind, rows, layer in ((0, LAYER, 2), (1, 2 * LAYER, 3)):
-                partial(kind, 0, j, rows, layer, 0).wait_send()
-                partial_stats(kind, 0, j, layer).wait_send()
+            partial(j, 2 * LAYER, 2).wait_send()
+            partial_stats(j, 2).wait_send()
 
         @pl.when(z == 2)
         def _():
-            partial(0, 1, j, LAYER, 3, LAYER).wait_send()
-            partial_stats(0, 1, j, 3).wait_send()
+            onward(j).wait_send()
+            partial(j, LAYER, 3).wait_send()
+            partial_stats(j, 3).wait_send()
 
         for d in (1, 2, 3):
             back(j, d).wait_send()
 
-        @pl.when(jnp.logical_not(stays))
+        @pl.when(jnp.logical_not(stays(j)))
         def _():
             back(j, 0).wait_send()
 
@@ -645,24 +684,23 @@
             pltpu.VMEM((3 * LAYER, cols, block), bf16),
             pltpu.VMEM((2 * LAYER, cols, block), bf16),
             pltpu.VMEM((blocks, 8, HD), f32),
-            pltpu.VMEM((2, blocks, 8, HD), f32),
+            pltpu.VMEM((blocks, 8, HD), f32),
             pltpu.VMEM((stride, block), bf16),
             pltpu.VMEM((2, half, local_feat), bf16),
             pltpu.VMEM((half, width), f32),
             pltpu.VMEM((depth, width), bf16),
             pltpu.VMEM((depth, width), bf16),
             pltpu.VMEM((half, width), bf16),
-            dma((7,)),
+            dma((4,)),
+            dma((3, CHUNKS)),
             dma((3 * CHUNKS, LAYER)),
             dma((3 * CHUNKS, LAYER)),
             dma((4 * CHUNKS, LAYER)),
             dma((4 * CHUNKS, LAYER)),
             dma((2, CHUNKS)),
             dma((2, CHUNKS)),
-            dma((2, CHUNKS)),
-            dma((2, CHUNKS)),
             dma((CHUNKS, LAYER)),
-            dma((2 * (half // cols), CHUNKS)),
+            dma((2 * LAYER, CHUNKS // 2)),
             dma((3, 8 * PIECES)),
             dma((8 * PIECES,)),
             dma,
@@ -764,7 +802,7 @@
         )
         for t in range(3)
     ]
-    local.append(pltpu.make_async_copy(w_hbm, w_own, local_sem.at[6]))
+    local.append(pltpu.make_async_copy(w_hbm, w_own, local_sem.at[3]))
     for copy in local:
         copy.start()
     for copy in local[:3]:

time: 115 us -> 108 us (0.939)
  Pallas kernels: 109 us -> 102 us
    pallas_call x1, Pallas kernels: 109 us -> 102 us  [call_layered(): pl.pallas_call(functools.partial(layered, n), out_shape=jax.ShapeDtypeStr...]
where the time goes in v3:
time: 108 us; the launch traced here: 107 us
  Pallas kernels  102 us (94%)
  local copies, waits for them, and re-layouts  4.7 us (4%)
    pallas_call x1, Pallas kernels, call_layered(): pl.pallas_call(functools.partial(layered, n), out_shape=jax.ShapeDtypeStr...  102 us
    unnamed x1, local copies, waits for them, and re-layouts  4.7 us

profile of v3, /device:TPU:25, one launch (start us, length us, event | category | flops | bytes accessed | tf_op | source)
XLA Modules:
  0.0 106.5 jit_solution(14907934206452483630)
XLA Ops:
  0.0 101.8 %shard_map.46 = bf16[512,4096]{1,0:T(8,128)(2,1)} custom-call(bf16[1,1024,1024]{2,1,0:T(8,128)(2,1)} %q_hbm.1, bf16[1,1024,1024]{2,1,0:T(8,128)(2,1)} %k_hbm.1, bf16[1,1024,1024]{2,1,0:T(8,128)(2,1)} %v_hbm.1, bf16[1024,4096]{1,0:T(8,128)(2,1)} %w_hbm.1), custom_call_target="tpu_custom_call" | custom-call | tf_op jit(solution)/shard_map/pallas_call | solution.py:674
  101.8 4.7 %copy.6 = bf16[1,512,4096]{2,1,0:T(8,128)(2,1)} copy(bf16[1,512,4096]{2,1,0:T(8,128)(2,1)} %bitcast.1) | data formatting | bytes 8388608

commit v4 on v3

--- a/solution.py
+++ b/solution.py
@@ -198,34 +198,21 @@
         w_copy(w_other, 2 * (1 - even) + q, core, k, 2, me, other).wait_recv()
         w_beside(q, k).start()
 
-    def exchange(ts):
-        @pl.loop(0, CHUNKS)
-        def _(j):
-            for t in ts:
-                for d in (2, 3, 1):
-                    lay(t, j, d, False).start()
-
-    for layer in routes:
-
-        @pl.when(z == layer)
-        def _():
-            for j in range(AHEAD):
-                direct(layer, j)
-
-    @pl.when(z < 2)
-    def _():
-        exchange((1, 2))
-        exchange((0,))
-
-    @pl.when(z >= 2)
-    def _():
-        exchange((0,))
-        exchange((1, 2))
-
-    @pl.loop(0, PIECES)
-    def _(k):
-        w_first(0, k).start()
-        w_first(1, k).start()
+    ready = pltpu.get_barrier_semaphore()
+
+    def greet(ctx, at):
+        pl.semaphore_signal(ready, 1, device_id=(ctx, at), device_id_type=MESH)
+
+    greet(me, other)
+    for d in (1, 2, 3):
+        greet(here(peers[d]), head)
+        greet(here(peers[d]), other)
+    for edge, towards in ((0, -LAYER), (LAYER - 1, LAYER)):
+
+        @pl.when(z != edge)
+        def _():
+            greet(here(s) + towards, head)
+            greet(here(sib) + towards, head)
 
     local = [
         pltpu.make_async_copy(hbm[t].at[0, :, pl.ds(0, block)], (q_row, k_row, v_row)[t], local_sem.at[t])
@@ -243,6 +230,39 @@
     local.append(pltpu.make_async_copy(w_hbm, w_own, local_sem.at[3]))
     for copy in local:
         copy.start()
+
+    inner = jnp.minimum(z, 1) + jnp.minimum(LAYER - 1 - z, 1)
+    pl.semaphore_wait(ready, 2 * LAYER - 1 + 2 * inner)
+
+    def exchange(ts):
+        @pl.loop(0, CHUNKS)
+        def _(j):
+            for t in ts:
+                for d in (2, 3, 1):
+                    lay(t, j, d, False).start()
+
+    for layer in routes:
+
+        @pl.when(z == layer)
+        def _():
+            for j in range(AHEAD):
+                direct(layer, j)
+
+    @pl.when(z < 2)
+    def _():
+        exchange((1, 2))
+        exchange((0,))
+
+    @pl.when(z >= 2)
+    def _():
+        exchange((0,))
+        exchange((1, 2))
+
+    @pl.loop(0, PIECES)
+    def _(k):
+        w_first(0, k).start()
+        w_first(1, k).start()
+
     for copy in local[:-1]:
         copy.wait()
 
@@ -470,14 +490,12 @@
 
     @pl.loop(0, CHUNKS)
     def _(j):
-        @pl.when(j < 2)
-        def _():
-            @pl.loop(j * (heads // 2), (j + 1) * (heads // 2))
-            def _(h):
-                for start in range(0, stride, tile):
-                    row_tile(h, start)
-
-        @pl.when(j == 1)
+        @pl.when(j < heads)
+        def _():
+            for start in range(0, stride, tile):
+                row_tile(j, start)
+
+        @pl.when(j == heads - 1)
         def _():
             row_copy.start()
             joined[head, :, pl.ds(0, block)] = row_out[pl.ds(pl.multiple_of(head * half, half), half)]
@@ -500,7 +518,7 @@
         def _():
             ext(j)
 
-        @pl.when(j == 2)
+        @pl.when(j == heads)
         def _():
             local[-1].wait()
             tiles(own_row_part)
@@ -529,25 +547,17 @@
 
     w_in(1, PIECES - 1)
 
-    @pl.when(z >= 2)
-    def _():
-        @pl.loop(CHUNKS // 2 - 1, CHUNKS - 2)
-        def _(c):
-            combine(c)
-
-    @pl.loop(0, PIECES)
-    def _(k):
-        w_on(0, k)
-
-    @pl.when(z >= 2)
-    def _():
-        @pl.loop(CHUNKS - 2, CHUNKS)
-        def _(c):
-            combine(c)
-
-    @pl.loop(0, PIECES // 2)
-    def _(k):
-        w_on(1, k)
+    def combine_some(first, last):
+        @pl.when(z >= 2)
+        def _():
+            @pl.loop(first, last)
+            def _(c):
+                combine(c)
+
+    def w_on_some(q, first, last):
+        @pl.loop(first, last)
+        def _(k):
+            w_on(q, k)
 
     def w_from_sibling(qs, first, last):
         @pl.loop(first, last)
@@ -555,9 +565,6 @@
             for q in qs:
                 w_copy(w_other, q, 1 - core, k, 1, here(sib), head).wait_recv()
 
-    w_from_sibling((0, 1, 2, 3), 0, PIECES // 2)
-    row_copy.wait_recv()
-
     def other_row_part(lanes):
         summed[:, lanes] += jnp.dot(
             joined[other, :, pl.ds(0, block)],
@@ -565,43 +572,59 @@
             preferred_element_type=jnp.float32,
         )
 
-    tiles(other_row_part)
-
-    def back_wait(source_head):
-        for slot in range(LAYER):
-
-            @pl.when(jnp.logical_not((slot == s) & (head == source_head)))
-            def _():
-                @pl.loop(0, CHUNKS // 2)
-                def _(i):
-                    remote(
-                        o_out.at[0, pl.ds(i * cw, cw)],
-                        joined.at[source_head, pl.ds(place(2 * i, slot), cw), feats],
-                        back_send.at[i, 0], back_recv.at[source_head * LAYER + slot, i],
-                        me, other,
-                    ).wait_recv()
-
-    back_wait(head)
-    back_wait(other)
-    w_from_sibling((2 * even, 2 * even + 1), PIECES // 2, PIECES)
+    def back_wait(u):
+        for source_head in (head, other):
+            for slot in range(LAYER):
+
+                @pl.when(jnp.logical_not((slot == s) & (head == source_head)))
+                def _():
+                    for i in range(u * CHUNKS // 4, (u + 1) * CHUNKS // 4):
+                        remote(
+                            o_out.at[0, pl.ds(0, cw)],
+                            joined.at[source_head, pl.ds(place(2 * i, slot), cw), feats],
+                            back_send.at[i, 0], back_recv.at[source_head * LAYER + slot, i],
+                            me, other,
+                        ).wait_recv()
+
     quarter = block // 2
     early = pl.ds(pl.multiple_of(block + even * quarter, quarter), quarter)
     late = pl.ds(pl.multiple_of(block + (1 - even) * quarter, quarter), quarter)
-
-    def col_part(lanes):
-        total = summed[:, lanes] + jnp.dot(
-            joined[head, :, feats], w_own[feats, lanes], preferred_element_type=jnp.float32
-        )
-        summed[:, lanes] = total + jnp.dot(
-            joined[other, :, early], w_other[early, lanes], preferred_element_type=jnp.float32
-        )
-
-    tiles(col_part)
-
-    @pl.loop(PIECES // 2, PIECES)
-    def _(k):
-        w_on(1, k)
-
+    run = CHUNKS // 4 * cw
+
+    def col_part(u):
+        rows = [pl.ds(slot * (cols // 2) + u * run, run) for slot in range(LAYER)]
+
+        def part(lanes):
+            total = jnp.dot(
+                jnp.concatenate([joined[head, at, feats] for at in rows]),
+                w_own[feats, lanes],
+                preferred_element_type=jnp.float32,
+            )
+            total += jnp.dot(
+                jnp.concatenate([joined[other, at, early] for at in rows]),
+                w_other[early, lanes],
+                preferred_element_type=jnp.float32,
+            )
+            for slot, at in enumerate(rows):
+                summed[at, lanes] += total[slot * run : (slot + 1) * run]
+
+        tiles(part)
+
+    combine_some(CHUNKS // 2 - 1, CHUNKS - 3)
+    w_on_some(0, 0, PIECES // 2)
+    w_on_some(1, 0, PIECES // 2)
+    combine_some(CHUNKS - 3, CHUNKS - 1)
+    w_from_sibling((0, 1, 2, 3), 0, PIECES // 2)
+    row_copy.wait_recv()
+    tiles(other_row_part)
+    combine_some(CHUNKS - 1, CHUNKS)
+    w_on_some(0, PIECES // 2, PIECES)
+    w_from_sibling((2 * even, 2 * even + 1), PIECES // 2, PIECES)
+    back_wait(0)
+    col_part(0)
+    back_wait(1)
+    col_part(1)
+    w_on_some(1, PIECES // 2, PIECES)
     w_from_sibling((2 - 2 * even, 3 - 2 * even), PIECES // 2, PIECES)
 
     def leave(c):
@@ -707,7 +730,9 @@
             dma,
             dma((width // 512,)),
         ],
-        compiler_params=pltpu.CompilerParams(has_side_effects=True, vmem_limit_bytes=60 * 2**20),
+        compiler_params=pltpu.CompilerParams(
+            collective_id=0, has_side_effects=True, vmem_limit_bytes=60 * 2**20
+        ),
     )(queries, keys, values, w_out)
 
 

time: 108 us -> 98.3 us (0.910); the launches traced: 107 us -> 98 us
  Pallas kernels: 102 us -> 93.3 us
    pallas_call x1, Pallas kernels: 102 us -> 93.3 us  [call_layered(): pl.pallas_call(functools.partial(layered, n), out_shape=jax.ShapeDtypeStr...]
where the time goes in v4:
time: 98.3 us; the launch traced here: 98 us
  Pallas kernels  93.3 us (95%)
  local copies, waits for them, and re-layouts  4.7 us (5%)
    pallas_call x1, Pallas kernels, call_layered(): pl.pallas_call(functools.partial(layered, n), out_shape=jax.ShapeDtypeStr...  93.3 us
    unnamed x1, local copies, waits for them, and re-layouts  4.7 us

profile of v4, /device:TPU:25, one launch (start us, length us, event | category | flops | bytes accessed | tf_op | source)
XLA Modules:
  0.0 98.0 jit_solution(10106569556618891759)
XLA Ops:
  0.0 93.3 %shard_map.46 = bf16[512,4096]{1,0:T(8,128)(2,1)} custom-call(bf16[1,1024,1024]{2,1,0:T(8,128)(2,1)} %q_hbm.1, bf16[1,1024,1024]{2,1,0:T(8,128)(2,1)} %k_hbm.1, bf16[1,1024,1024]{2,1,0:T(8,128)(2,1)} %v_hbm.1, bf16[1024,4096]{1,0:T(8,128)(2,1)} %w_hbm.1), custom_call_target="tpu_custom_call" | custom-call | tf_op jit(solution)/shard_map/pallas_call | solution.py:697
  93.3 4.7 %copy.6 = bf16[1,512,4096]{2,1,0:T(8,128)(2,1)} copy(bf16[1,512,4096]{2,1,0:T(8,128)(2,1)} %bitcast.1) | data formatting | bytes 8388608

commit v5 on v4

--- a/solution.py
+++ b/solution.py
@@ -171,11 +171,17 @@
     z_next = me + LAYER - 2 * LAYER * lax.rem(z, 2)
     z_early = (z == 1) | (z == 2)
 
+    def to_side(k):
+        return (z > 0) | (k < PIECES // 2)
+
     def w_first(q, k):
         return w_copy(w_hbm, 2 * even + q, core, k, 0, me, other)
 
     def w_side(q, k):
         return w_copy(w_other, 2 * even + q, core, k, 2, y_next if q == 0 else z_next, head)
+
+    def w_extra(k):
+        return w_copy(w_other, 2 * even + 1, core, k, 3, me - LAYER, head)
 
     def w_beside(q, k):
         return w_copy(w_other, 2 * (1 - even) + q, core, k, 1, here(sib), head)
@@ -190,9 +196,26 @@
             w_side(q, k).start()
         else:
 
-            @pl.when(z_early | (k > 0))
+            @pl.when(z_early)
             def _():
                 w_side(q, k).start()
+
+            @pl.when((z == 2) & (k >= PIECES // 2))
+            def _():
+                w_extra(k).start()
+
+    def w_step(i):
+        high = z >= 2
+        for_z = jnp.where(high, jnp.where(i < PIECES, 1, 0), lax.rem(i, 2))
+        k = jnp.where(high, lax.rem(i, PIECES), lax.div(i, 2))
+
+        @pl.when(for_z == 1)
+        def _():
+            w_in(1, k)
+
+        @pl.when(for_z == 0)
+        def _():
+            w_in(0, k)
 
     def w_on(q, k):
         w_copy(w_other, 2 * (1 - even) + q, core, k, 2, me, other).wait_recv()
@@ -258,10 +281,20 @@
         exchange((0,))
         exchange((1, 2))
 
-    @pl.loop(0, PIECES)
-    def _(k):
-        w_first(0, k).start()
-        w_first(1, k).start()
+    @pl.when(z < 2)
+    def _():
+        @pl.loop(0, PIECES)
+        def _(k):
+            w_first(0, k).start()
+            w_first(1, k).start()
+
+    @pl.when(z >= 2)
+    def _():
+        for q in (1, 0):
+
+            @pl.loop(0, PIECES)
+            def _(k):
+                w_first(q, k).start()
 
     for copy in local[:-1]:
         copy.wait()
@@ -474,7 +507,7 @@
         joined.at[head, :, pl.ds(0, block)], row_send, row_recv, me, other,
     )
     step = 512
-    count = staged.shape[1] // step
+    count = w_own.shape[1] // step
 
     def tiles(add):
         @pl.loop(0, count)
@@ -523,17 +556,19 @@
             local[-1].wait()
             tiles(own_row_part)
 
-        @pl.when(jnp.logical_not(z_early) & (j == CHUNKS // 2))
-        def _():
-            w_side(1, 0).start()
-
-        @pl.when((j > 0) & (lax.rem(j, 2) == 1))
-        def _():
-            w_in(0, lax.div(j, 2))
-
-        @pl.when((j > 0) & (lax.rem(j, 2) == 0))
-        def _():
-            w_in(1, lax.div(j, 2) - 1)
+        i = j - jnp.where(z == 1, 0, 1)
+
+        @pl.when(i >= 0)
+        def _():
+            w_step(i)
+
+        @pl.when(jnp.logical_not(z_early) & (j == PIECES))
+        def _():
+            @pl.loop(0, PIECES)
+            def _(k):
+                @pl.when(to_side(k))
+                def _():
+                    w_side(1, k).start()
 
         @pl.when(j >= CHUNKS // 2)
         def _():
@@ -541,14 +576,18 @@
             own(c)
             own(c + 1)
 
-            @pl.when((z >= 2) & (j > CHUNKS // 2))
+            lag = z - 2
+
+            @pl.when((z >= 2) & (j >= CHUNKS // 2 + lag))
             def _():
-                combine(j - CHUNKS // 2 - 1)
-
-    w_in(1, PIECES - 1)
-
-    def combine_some(first, last):
-        @pl.when(z >= 2)
+                combine(j - CHUNKS // 2 - lag)
+
+    @pl.when(z != 1)
+    def _():
+        w_step(2 * PIECES - 1)
+
+    def combine_some(layer, first, last):
+        @pl.when(z == layer)
         def _():
             @pl.loop(first, last)
             def _(c):
@@ -586,59 +625,51 @@
                             me, other,
                         ).wait_recv()
 
-    quarter = block // 2
-    early = pl.ds(pl.multiple_of(block + even * quarter, quarter), quarter)
-    late = pl.ds(pl.multiple_of(block + (1 - even) * quarter, quarter), quarter)
     run = CHUNKS // 4 * cw
 
-    def col_part(u):
+    def leave(u, c):
+        lanes = pl.ds(pl.multiple_of(c * step, step), step)
+        return pltpu.make_async_copy(
+            staged.at[:, u, :, lanes], out_hbm.at[:, u, :, lanes], out_sem.at[u, c]
+        )
+
+    def finish(u):
         rows = [pl.ds(slot * (cols // 2) + u * run, run) for slot in range(LAYER)]
 
-        def part(lanes):
+        @pl.loop(0, count)
+        def _(c):
+            lanes = pl.ds(pl.multiple_of(c * step, step), step)
             total = jnp.dot(
                 jnp.concatenate([joined[head, at, feats] for at in rows]),
                 w_own[feats, lanes],
                 preferred_element_type=jnp.float32,
             )
             total += jnp.dot(
-                jnp.concatenate([joined[other, at, early] for at in rows]),
-                w_other[early, lanes],
+                jnp.concatenate([joined[other, at, feats] for at in rows]),
+                w_other[feats, lanes],
                 preferred_element_type=jnp.float32,
             )
             for slot, at in enumerate(rows):
-                summed[at, lanes] += total[slot * run : (slot + 1) * run]
-
-        tiles(part)
-
-    combine_some(CHUNKS // 2 - 1, CHUNKS - 3)
+                part = summed[at, lanes] + total[slot * run : (slot + 1) * run]
+                staged[slot, u, :, lanes] = part.astype(jnp.bfloat16)
+            leave(u, c).start()
+
+    combine_some(2, CHUNKS // 2, CHUNKS)
+    combine_some(3, CHUNKS // 2 - 1, CHUNKS - 3)
     w_on_some(0, 0, PIECES // 2)
     w_on_some(1, 0, PIECES // 2)
-    combine_some(CHUNKS - 3, CHUNKS - 1)
+    combine_some(3, CHUNKS - 3, CHUNKS - 1)
     w_from_sibling((0, 1, 2, 3), 0, PIECES // 2)
     row_copy.wait_recv()
     tiles(other_row_part)
-    combine_some(CHUNKS - 1, CHUNKS)
+    combine_some(3, CHUNKS - 1, CHUNKS)
     w_on_some(0, PIECES // 2, PIECES)
-    w_from_sibling((2 * even, 2 * even + 1), PIECES // 2, PIECES)
+    w_on_some(1, PIECES // 2, PIECES)
+    w_from_sibling((0, 1, 2, 3), PIECES // 2, PIECES)
     back_wait(0)
-    col_part(0)
+    finish(0)
     back_wait(1)
-    col_part(1)
-    w_on_some(1, PIECES // 2, PIECES)
-    w_from_sibling((2 - 2 * even, 3 - 2 * even), PIECES // 2, PIECES)
-
-    def leave(c):
-        lanes = pl.ds(pl.multiple_of(c * step, step), step)
-        return pltpu.make_async_copy(staged.at[:, lanes], out_hbm.at[:, lanes], out_sem.at[c])
-
-    @pl.loop(0, count)
-    def _(c):
-        lanes = pl.ds(pl.multiple_of(c * step, step), step)
-        total = summed[:, lanes] + jnp.dot(
-            joined[other, :, late], w_other[late, lanes], preferred_element_type=jnp.float32
-        )
-        staged[:, lanes] = total.astype(jnp.bfloat16)
-        leave(c).start()
+    finish(1)
 
     @pl.loop(0, CHUNKS)
     def _(j):
@@ -676,14 +707,23 @@
         for q in (0, 1):
             w_first(q, k).wait_send()
             w_here(q, k).wait_send()
-            w_side(q, k).wait_send()
             w_beside(q, k).wait_send()
+        w_side(0, k).wait_send()
+
+        @pl.when(to_side(k))
+        def _():
+            w_side(1, k).wait_send()
+
+        @pl.when((z == 2) & (k >= PIECES // 2))
+        def _():
+            w_extra(k).wait_send()
 
     row_copy.wait_send()
 
     @pl.loop(0, count)
     def _(c):
-        leave(c).wait()
+        leave(0, c).wait()
+        leave(1, c).wait()
 
 
 def call_layered(n, queries, keys, values, w_out, half):
@@ -696,7 +736,7 @@
     blocks = cols // WIDTH
     return pl.pallas_call(
         functools.partial(layered, n),
-        out_shape=jax.ShapeDtypeStruct((half, width), bf16),
+        out_shape=jax.ShapeDtypeStruct((LAYER, 2, half // (2 * LAYER), width), bf16),
         in_specs=[pl.BlockSpec(memory_space=pltpu.HBM)] * 4,
         out_specs=pl.BlockSpec(memory_space=pltpu.HBM),
         scratch_shapes=[pltpu.VMEM((stride, block), bf16)] * 3
@@ -713,7 +753,7 @@
             pltpu.VMEM((half, width), f32),
             pltpu.VMEM((depth, width), bf16),
             pltpu.VMEM((depth, width), bf16),
-            pltpu.VMEM((half, width), bf16),
+            pltpu.VMEM((LAYER, 2, half // (2 * LAYER), width), bf16),
             dma((4,)),
             dma((3, CHUNKS)),
             dma((3 * CHUNKS, LAYER)),
@@ -724,11 +764,11 @@
             dma((2, CHUNKS)),
             dma((CHUNKS, LAYER)),
             dma((2 * LAYER, CHUNKS // 2)),
-            dma((3, 8 * PIECES)),
+            dma((4, 8 * PIECES)),
             dma((8 * PIECES,)),
             dma,
             dma,
-            dma((width // 512,)),
+            dma((2, width // 512)),
         ],
         compiler_params=pltpu.CompilerParams(
             collective_id=0, has_side_effects=True, vmem_limit_bytes=60 * 2**20

time: 98.3 us -> 94.4 us (0.960)
  Pallas kernels: 93.3 us -> 89.5 us
    pallas_call x1, Pallas kernels: 93.3 us -> 89.5 us  [call_layered(): pl.pallas_call(functools.partial(layered, n), out_shape=jax.ShapeDtypeStr...]
where the time goes in v5:
time: 94.4 us; the launch traced here: 94.3 us
  Pallas kernels  89.5 us (95%)
  local copies, waits for them, and re-layouts  4.7 us (5%)
    pallas_call x1, Pallas kernels, call_layered(): pl.pallas_call(functools.partial(layered, n), out_shape=jax.ShapeDtypeStr...  89.5 us
    unnamed x1, local copies, waits for them, and re-layouts  4.7 us

profile of v5, /device:TPU:25, one launch (start us, length us, event | category | flops | bytes accessed | tf_op | source)
XLA Modules:
  0.0 94.3 jit_solution(2569182494822338531)
XLA Ops:
  0.0 89.5 %shard_map.46 = bf16[4,2,64,4096]{3,2,1,0:T(8,128)(2,1)} custom-call(bf16[1,1024,1024]{2,1,0:T(8,128)(2,1)} %q_hbm.1, bf16[1,1024,1024]{2,1,0:T(8,128)(2,1)} %k_hbm.1, bf16[1,1024,1024]{2,1,0:T(8,128)(2,1)} %v_hbm.1, bf16[1024,4096]{1,0:T(8,128)(2,1)} %w_hbm.1), custom_call_target="tpu_custom_call" | custom-call | tf_op jit(solution)/shard_map/pallas_call | solution.py:737
  89.6 4.7 %copy.6 = bf16[1,512,4096]{2,1,0:T(8,128)(2,1)} copy(bf16[1,512,4096]{2,1,0:T(8,128)(2,1)} %bitcast.1) | data formatting | bytes 8388608

commit v6 on v5

--- a/solution.py
+++ b/solution.py
@@ -55,10 +55,10 @@
 
 
 def layered(
-    n, q_hbm, k_hbm, v_hbm, w_hbm, out_hbm, q_row, k_row, v_row, q_in, k_in, v_in, o_out, p_in,
-    stats, stats_in, row_out, joined, summed, w_own, w_other, staged,
+    n, q_hbm, k_hbm, v_hbm, w_hbm, staged, q_row, k_row, v_row, q_in, k_in, v_in, o_out, p_in,
+    stats, stats_in, row_out, joined, summed, w_own, w_other,
     local_sem, chunk_sem, lay_send, lay_recv, up_send, up_recv, part_send, part_recv,
-    back_send, back_recv, w_send, w_recv, row_send, row_recv, out_sem,
+    back_send, back_recv, w_send, w_recv, row_send, row_recv,
 ):
     me, head = lax.axis_index("ctx"), lax.axis_index("head")
     other = 1 - head
@@ -627,12 +627,6 @@
 
     run = CHUNKS // 4 * cw
 
-    def leave(u, c):
-        lanes = pl.ds(pl.multiple_of(c * step, step), step)
-        return pltpu.make_async_copy(
-            staged.at[:, u, :, lanes], out_hbm.at[:, u, :, lanes], out_sem.at[u, c]
-        )
-
     def finish(u):
         rows = [pl.ds(slot * (cols // 2) + u * run, run) for slot in range(LAYER)]
 
@@ -652,7 +646,6 @@
             for slot, at in enumerate(rows):
                 part = summed[at, lanes] + total[slot * run : (slot + 1) * run]
                 staged[slot, u, :, lanes] = part.astype(jnp.bfloat16)
-            leave(u, c).start()
 
     combine_some(2, CHUNKS // 2, CHUNKS)
     combine_some(3, CHUNKS // 2 - 1, CHUNKS - 3)
@@ -720,11 +713,6 @@
 
     row_copy.wait_send()
 
-    @pl.loop(0, count)
-    def _(c):
-        leave(0, c).wait()
-        leave(1, c).wait()
-
 
 def call_layered(n, queries, keys, values, w_out, half):
     _, stride, local_feat = queries.shape
@@ -736,9 +724,9 @@
     blocks = cols // WIDTH
     return pl.pallas_call(
         functools.partial(layered, n),
-        out_shape=jax.ShapeDtypeStruct((LAYER, 2, half // (2 * LAYER), width), bf16),
+        out_shape=pltpu.VMEM((LAYER, 2, half // (2 * LAYER), width), bf16),
         in_specs=[pl.BlockSpec(memory_space=pltpu.HBM)] * 4,
-        out_specs=pl.BlockSpec(memory_space=pltpu.HBM),
+        out_specs=pl.BlockSpec(memory_space=pltpu.VMEM),
         scratch_shapes=[pltpu.VMEM((stride, block), bf16)] * 3
         + [
             pltpu.VMEM((3 * LAYER, cols, block), bf16),
@@ -753,7 +741,6 @@
             pltpu.VMEM((half, width), f32),
             pltpu.VMEM((depth, width), bf16),
             pltpu.VMEM((depth, width), bf16),
-            pltpu.VMEM((LAYER, 2, half // (2 * LAYER), width), bf16),
             dma((4,)),
             dma((3, CHUNKS)),
             dma((3 * CHUNKS, LAYER)),
@@ -768,10 +755,9 @@
             dma((8 * PIECES,)),
             dma,
             dma,
-            dma((2, width // 512)),
         ],
         compiler_params=pltpu.CompilerParams(
-            collective_id=0, has_side_effects=True, vmem_limit_bytes=60 * 2**20
+            collective_id=0, has_side_effects=True, vmem_limit_bytes=56 * 2**20
         ),
     )(queries, keys, values, w_out)
 

time: 94.4 us -> 91.4 us (0.968)
  local copies, waits for them, and re-layouts: 4.7 us -> 2.02 us
    unnamed x1, local copies, waits for them, and re-layouts: 4.7 us -> 2.02 us
where the time goes in v6:
time: 91.4 us; the launch traced here: 91.3 us
  Pallas kernels  89.3 us (98%)
  local copies, waits for them, and re-layouts  2.02 us (2%)
    pallas_call x1, Pallas kernels, call_layered(): pl.pallas_call(functools.partial(layered, n), out_shape=pltpu.VMEM((LAYER...  89.3 us
    unnamed x1, local copies, waits for them, and re-layouts  2.02 us

profile of v6, /device:TPU:25, one launch (start us, length us, event | category | flops | bytes accessed | tf_op | source)
XLA Modules:
  0.0 91.3 jit_solution(16555535971198345864)
XLA Ops:
  0.0 89.3 %shard_map.46 = bf16[4,2,64,4096]{3,2,1,0:T(8,128)(2,1)S(1)} custom-call(bf16[1,1024,1024]{2,1,0:T(8,128)(2,1)} %q_hbm.1, bf16[1,1024,1024]{2,1,0:T(8,128)(2,1)} %k_hbm.1, bf16[1,1024,1024]{2,1,0:T(8,128)(2,1)} %v_hbm.1, bf16[1024,4096]{1,0:T(8,128)(2,1)} %w_hbm.1), custom_call_target="tpu_custom_call" | custom-call | tf_op jit(solution)/shard_map/pallas_call | solution.py:725
  89.3 2.0 %copy.6 = bf16[1,512,4096]{2,1,0:T(8,128)(2,1)} copy(bf16[1,512,4096]{2,1,0:T(8,128)(2,1)S(1)} %bitcast.1) | data formatting | bytes 8388608

commit v7 on v6

--- a/solution.py
+++ b/solution.py
@@ -506,7 +506,7 @@
         row_out.at[pl.ds(pl.multiple_of(other * half, half), half)],
         joined.at[head, :, pl.ds(0, block)], row_send, row_recv, me, other,
     )
-    step = 512
+    step = 2048
     count = w_own.shape[1] // step
 
     def tiles(add):

time: 91.4 us -> 89.3 us (0.977)
  Pallas kernels: 89.3 us -> 87.1 us
    pallas_call x1, Pallas kernels: 89.3 us -> 87.1 us  [call_layered(): pl.pallas_call(functools.partial(layered, n), out_shape=pltpu.VMEM((LAYER...]
where the time goes in v7:
time: 89.3 us; the launch traced here: 89.2 us
  Pallas kernels  87.1 us (98%)
  local copies, waits for them, and re-layouts  2.02 us (2%)
    pallas_call x1, Pallas kernels, call_layered(): pl.pallas_call(functools.partial(layered, n), out_shape=pltpu.VMEM((LAYER...  87.1 us
    unnamed x1, local copies, waits for them, and re-layouts  2.02 us

profile of v7, /device:TPU:25, one launch (start us, length us, event | category | flops | bytes accessed | tf_op | source)
XLA Modules:
  0.0 89.2 jit_solution(6629859311555280645)
XLA Ops:
  0.0 87.1 %shard_map.46 = bf16[4,2,64,4096]{3,2,1,0:T(8,128)(2,1)S(1)} custom-call(bf16[1,1024,1024]{2,1,0:T(8,128)(2,1)} %q_hbm.1, bf16[1,1024,1024]{2,1,0:T(8,128)(2,1)} %k_hbm.1, bf16[1,1024,1024]{2,1,0:T(8,128)(2,1)} %v_hbm.1, bf16[1024,4096]{1,0:T(8,128)(2,1)} %w_hbm.1), custom_call_target="tpu_custom_call" | custom-call | tf_op jit(solution)/shard_map/pallas_call | solution.py:725
  87.1 2.0 %copy.6 = bf16[1,512,4096]{2,1,0:T(8,128)(2,1)} copy(bf16[1,512,4096]{2,1,0:T(8,128)(2,1)S(1)} %bitcast.1) | data formatting | bytes 8388608

commit v8 on v7

--- a/solution.py
+++ b/solution.py
@@ -506,7 +506,7 @@
         row_out.at[pl.ds(pl.multiple_of(other * half, half), half)],
         joined.at[head, :, pl.ds(0, block)], row_send, row_recv, me, other,
     )
-    step = 2048
+    step = 4096
     count = w_own.shape[1] // step
 
     def tiles(add):

time: 89.3 us -> 89 us (level)
  no operation moved by 1% of the time
where the time goes in v8:
time: 89 us; the launch traced here: 88.8 us
  Pallas kernels  86.8 us (98%)
  local copies, waits for them, and re-layouts  2.02 us (2%)
    pallas_call x1, Pallas kernels, call_layered(): pl.pallas_call(functools.partial(layered, n), out_shape=pltpu.VMEM((LAYER...  86.8 us
    unnamed x1, local copies, waits for them, and re-layouts  2.02 us

profile of v8, /device:TPU:25, one launch (start us, length us, event | category | flops | bytes accessed | tf_op | source)
XLA Modules:
  0.0 88.8 jit_solution(12625415777091103756)
XLA Ops:
  0.0 86.8 %shard_map.46 = bf16[4,2,64,4096]{3,2,1,0:T(8,128)(2,1)S(1)} custom-call(bf16[1,1024,1024]{2,1,0:T(8,128)(2,1)} %q_hbm.1, bf16[1,1024,1024]{2,1,0:T(8,128)(2,1)} %k_hbm.1, bf16[1,1024,1024]{2,1,0:T(8,128)(2,1)} %v_hbm.1, bf16[1024,4096]{1,0:T(8,128)(2,1)} %w_hbm.1), custom_call_target="tpu_custom_call" | custom-call | tf_op jit(solution)/shard_map/pallas_call | solution.py:725
  86.8 2.0 %copy.6 = bf16[1,512,4096]{2,1,0:T(8,128)(2,1)} copy(bf16[1,512,4096]{2,1,0:T(8,128)(2,1)S(1)} %bitcast.1) | data formatting | bytes 8388608
